TPU v7x, 32 devices: a whole 2x2x4 slice. The times are simulated.
32 devices in a mesh: sp: 32 (over z, y, x, core).
Axes of the slice: x: 2, y: 2, z: 4, core: 2. Of those that a mesh axis runs over, the one named last changes fastest.
Arguments:
- x: bfloat16 [4, 4096, 2048], P(None, 'sp')
- d_y: bfloat16 [4, 4096, 2048], P(None, 'sp')
- ln_gamma: bfloat16 [2048], replicated
- ln_beta: bfloat16 [2048], replicated
- w_qkv: bfloat16 [2048, 6144], replicated
- b_qkv: bfloat16 [6144], replicated
- w_out: bfloat16 [2048, 2048], replicated
- b_out: bfloat16 [2048], replicated
- head_kind: int32 [32], replicated
Outputs:
- output 1: bfloat16 [4, 4096, 2048], P(None, 'sp')
- output 2: bfloat16 [4, 4096, 2048], P(None, 'sp')
- output 3: float32 [2048], replicated
- output 4: float32 [2048], replicated
- output 5: float32 [2048, 6144], replicated
- output 6: float32 [6144], replicated
- output 7: float32 [2048, 2048], replicated
- output 8: float32 [2048], replicated
All inputs are finite; a program needn't handle non-finite values.
Results may differ from a plain program's by a relative error of at most 0.0126655.
Values are sent between devices in bfloat16 or wider.
A program may use at most 1 GiB of HBM per device.

v0:
```python
import math
import jax
import jax.numpy as jnp
from jax import lax
from jax.sharding import PartitionSpec as P

LN_EPS = 1e-5
NEG_BIG = -1e30


def layer_norm(x_rows, gamma_f, beta_f):
    row_mean = jnp.mean(x_rows, axis=-1, keepdims=True)
    centred = x_rows - row_mean
    row_var = jnp.mean(centred * centred, axis=-1, keepdims=True)
    return centred * lax.rsqrt(row_var + LN_EPS) * gamma_f + beta_f


def score_probs(q_part, k_all, banded, q_first, band_width):
    q_len = q_part.shape[2]
    k_len = k_all.shape[2]
    score_scale = 1.0 / math.sqrt(q_part.shape[3])
    logits = jnp.einsum("bhqd,bhkd->bhqk", q_part, k_all, preferred_element_type=jnp.float32) * score_scale
    query_pos = q_first + lax.broadcasted_iota(jnp.int32, (1, 1, q_len, 1), 2)
    key_pos = lax.broadcasted_iota(jnp.int32, (1, 1, 1, k_len), 3)
    is_banded = (banded == 1)[None, :, None, None]
    allowed = (key_pos <= query_pos) & (jnp.logical_not(is_banded) | (key_pos > query_pos - band_width))
    return jax.nn.softmax(jnp.where(allowed, logits, NEG_BIG), axis=-1)


def attend_forward(q_all, k_all, v_all, banded, q_offset, band_width):
    q_len = q_all.shape[2]
    q_blk = min(128, q_len)

    def q_step(blk_index, out_buf):
        q_start = blk_index * q_blk
        q_part = lax.dynamic_slice_in_dim(q_all, q_start, q_blk, axis=2)
        attn_prob = score_probs(q_part, k_all, banded, q_offset + q_start, band_width)
        o_part = jnp.einsum("bhqk,bhkd->bhqd", attn_prob.astype(jnp.bfloat16), v_all, preferred_element_type=jnp.float32)
        return lax.dynamic_update_slice_in_dim(out_buf, o_part.astype(jnp.bfloat16), q_start, axis=2)

    return lax.fori_loop(0, q_len // q_blk, q_step, jnp.zeros_like(q_all))


def attend_backward(q_all, k_all, v_all, d_out, banded, q_offset, band_width):
    q_len = q_all.shape[2]
    q_blk = min(128, q_len)
    score_scale = 1.0 / math.sqrt(q_all.shape[3])

    def q_step(blk_index, grad_state):
        dq_buf, dk_acc, dv_acc = grad_state
        q_start = blk_index * q_blk
        q_part = lax.dynamic_slice_in_dim(q_all, q_start, q_blk, axis=2)
        do_part = lax.dynamic_slice_in_dim(d_out, q_start, q_blk, axis=2)
        attn_prob = score_probs(q_part, k_all, banded, q_offset + q_start, band_width)
        prob_bf = attn_prob.astype(jnp.bfloat16)
        d_prob = jnp.einsum("bhqd,bhkd->bhqk", do_part, v_all, preferred_element_type=jnp.float32).astype(jnp.bfloat16).astype(jnp.float32)
        d_logit = (attn_prob * (d_prob - jnp.sum(attn_prob * d_prob, axis=-1, keepdims=True)) * score_scale).astype(jnp.bfloat16)
        dq_part = jnp.einsum("bhqk,bhkd->bhqd", d_logit, k_all, preferred_element_type=jnp.float32)
        dk_acc = dk_acc + jnp.einsum("bhqk,bhqd->bhkd", d_logit, q_part, preferred_element_type=jnp.float32)
        dv_acc = dv_acc + jnp.einsum("bhqk,bhqd->bhkd", prob_bf, do_part, preferred_element_type=jnp.float32)
        dq_buf = lax.dynamic_update_slice_in_dim(dq_buf, dq_part.astype(jnp.bfloat16), q_start, axis=2)
        return dq_buf, dk_acc, dv_acc

    init_state = (jnp.zeros_like(q_all), jnp.zeros(k_all.shape, jnp.float32), jnp.zeros(v_all.shape, jnp.float32))
    return lax.fori_loop(0, q_len // q_blk, q_step, init_state)


def solution(mesh):
    seq_par = mesh.shape["sp"]
    tok_spec = P(None, "sp", None)

    def local_block(x, d_y, ln_gamma, ln_beta, w_qkv, b_qkv, w_out, b_out, head_kind):
        local_len = x.shape[1]
        d_model = x.shape[2]
        num_heads = head_kind.shape[0]
        head_dim = d_model // num_heads
        local_heads = num_heads // seq_par
        band_width = local_len * seq_par // 4
        my_kinds = lax.dynamic_slice_in_dim(head_kind, lax.axis_index("sp") * local_heads, local_heads)
        wqkv_r = w_qkv.reshape(d_model, 3, num_heads, head_dim)
        wout_r = w_out.reshape(num_heads, head_dim, d_model)
        x_f = x.astype(jnp.float32)
        h_f, ln_pull = jax.vjp(layer_norm, x_f, ln_gamma.astype(jnp.float32), ln_beta.astype(jnp.float32))
        h_norm = h_f.astype(jnp.bfloat16)
        qkv_bias = b_qkv.astype(jnp.float32).reshape(3, 1, num_heads, 1, head_dim)
        qkv_tok = (jnp.einsum("bsi,itnd->tbnsd", h_norm, wqkv_r, preferred_element_type=jnp.float32) + qkv_bias).astype(jnp.bfloat16)
        qkv_head = lax.all_to_all(qkv_tok, "sp", 2, 3, tiled=True)
        attn_head = attend_forward(qkv_head[0], qkv_head[1], qkv_head[2], my_kinds, 0, band_width)
        attn_tok = lax.all_to_all(attn_head, "sp", 2, 1, tiled=True)
        proj_out = jnp.einsum("bnsd,ndj->bsj", attn_tok, wout_r, preferred_element_type=jnp.float32)
        y_out = (x_f + proj_out + b_out.astype(jnp.float32)).astype(jnp.bfloat16)
        d_attn_tok = jnp.einsum("bsj,ndj->bnsd", d_y, wout_r, preferred_element_type=jnp.float32).astype(jnp.bfloat16)
        d_attn_head = lax.all_to_all(d_attn_tok, "sp", 1, 2, tiled=True)
        dq_head, dk_head, dv_head = attend_backward(qkv_head[0], qkv_head[1], qkv_head[2], d_attn_head, my_kinds, 0, band_width)
        d_qkv_head = jnp.stack([dq_head, dk_head.astype(jnp.bfloat16), dv_head.astype(jnp.bfloat16)])
        d_qkv_tok = lax.all_to_all(d_qkv_head, "sp", 3, 2, tiled=True)
        d_wqkv = jnp.einsum("bsi,tbnsd->itnd", h_norm, d_qkv_tok, preferred_element_type=jnp.float32).reshape(d_model, 3 * d_model)
        d_bqkv = jnp.sum(d_qkv_tok, axis=(1, 3), dtype=jnp.float32).reshape(3 * d_model)
        d_h = jnp.einsum("tbnsd,itnd->bsi", d_qkv_tok, wqkv_r, preferred_element_type=jnp.float32).astype(jnp.bfloat16).astype(jnp.float32)
        d_x_ln, d_gamma, d_beta = ln_pull(d_h)
        d_x = (d_y.astype(jnp.float32) + d_x_ln).astype(jnp.bfloat16)
        d_wout = jnp.einsum("bnsd,bsj->ndj", attn_tok, d_y, preferred_element_type=jnp.float32).reshape(d_model, d_model)
        d_bout = jnp.sum(d_y, axis=(0, 1), dtype=jnp.float32)
        grad_sums = lax.psum((d_gamma, d_beta, d_wqkv, d_bqkv, d_wout, d_bout), "sp")
        return (y_out, d_x) + tuple(grad_sums)

    return jax.shard_map(local_block, mesh=mesh, in_specs=(tok_spec, tok_spec, P(), P(), P(), P(), P(), P(), P()), out_specs=(tok_spec, tok_spec, P(), P(), P(), P(), P(), P()), check_vma=False)
```

profile of v0, /device:TPU:0, one launch (start us, length us, event | category | flops | bytes accessed | tf_op | source)
XLA Modules:
  0.0 3556.1 jit_solution(13561038791610604194)
XLA Ops:
  25.1 31.0 copy.86
  56.1 18.2 fusion.105
  78.6 16.6 all-to-all-start
  101.8 125.1 %all-to-all-done = bf16[3,4,32,128,64]{3,4,0,1,2:T(8,128)(2,1)} async-done(((bf16[3,4,32,128,64]{3,4,0,1,2:T(8,128)(2,1)}), bf16[3,4,32,128,64]{3,4,0,1,2:T(8,128)(2,1)}, u32[]{:S(2)}, u32[]{:S(2)}) %all-to-all-start) | async-done | bytes 6291488 | tf_op jit(solution)/shard_map/all_to_all | solution.py:87
  258.6 456.1 %while.35 = (s32[]{:T(128)}, bf16[4,1,4096,64]{2,3,0,1:T(8,128)(2,1)}, pred[1,1,1,1]{3,2,1,0:T(4,128)(4,1)}, bf16[4,1,4096,64]{2,3,0,1:T(8,128)(2,1)}, bf16[4,1,...) while((s32[]{:T(128)}, ...), condition=%wide.region_5.6_spmd, body=%wide.region_2.5_spmd.sunk | while | flops 551588096 | bytes 22157472 | solution.py:41
  742.9 1526.5 %while.36 = (s32[]{:T(128)}, bf16[4,1,4096,64]{2,3,0,1:T(8,128)(2,1)}, f32[4,1,4096,64]{2,3,0,1:T(8,128)}, f32[4,1,4096,64]{2,3,0,1:T(8,128)}, pred[1,1,1,1]{3,2...) while((s32[]{:T(128)}, ...), condition=%wide.region_10.11_spmd.clone, body=%wide.region_6.10_spmd.clone.sunk | while | flops 1400943872 | bytes 95762640 | solution.py:65
  813.3 15.1 fusion.188
  956.6 15.1 fusion.188
  1386.7 15.1 fusion.188
  1482.2 15.1 fusion.188
  1816.6 15.1 fusion.188
  1912.1 15.1 fusion.188
  2151.0 15.1 fusion.188
  2246.6 15.1 fusion.188
  2304.8 24.1 reshape.407
  2360.8 106.8 %all-to-all-done.3 = bf16[32,2,49152]{2,1,0:T(2,128)(2,1)} async-done(((bf16[32,2,49152]{2,1,0:T(2,128)(2,1)}), bf16[32,2,49152]{2,1,0:T(2,128)(2,1)}, u32[]{:S(2)}, u32[]{:S(2)}) %all-to-all-start.3) | async-done | bytes 6291488 | tf_op jit(solution)/shard_map/all_to_all | solution.py:96
  2467.6 23.5 reshape.408
  2491.1 18.6 copy.116
  2509.7 23.9 convolution_bitcast_fusion.2
  2567.6 18.5 copy.102
  2595.6 30.8 convert_reduce_fusion.1
  2633.7 46.2 %all-reduce = (f32[2048]{0:T(1024)}, f32[2048]{0:T(1024)}, f32[6144]{0:T(1024)}, f32[2048]{0:T(1024)}) all-reduce(f32[2048]{0:T(1024)S(1)} %get-tuple-element.424, f32[2048]{0:T(1024)S(1)} %get-tuple-element.426, f32[6144]{0:T(1024)S(1)} %reshape.389, f32[2048]{0:T(1024)S(1)} %get-tuple-element.475), channel_id=1, replica_groups=mesh['sp'=32] {'sp'}, use_global_device_ids=true, to_apply=%region_14.15 | all-reduce | flops 12288 | bytes 98304 | tf_op jit(solution)/shard_map/psum | solution.py:104
  2679.9 822.9 %all-reduce.4.cloned.1.call-done = (f32[2048,6144]{1,0:T(8,128)}, f32[2048,2048]{1,0:T(8,128)}) async-done(((f32[2048,6144]{1,0:T(8,128)}, f32[2048,2048]{1,0:T(8,128)}), (f32[2048,6144]{1,0:T(8,128)}, f32[2048,2048]{1,0:T(8,128)})) %all-reduce.4.cloned.1.call-update) | async-done | bytes 67108880 | tf_op jit(solution)/shard_map/psum | solution.py:104
  3502.8 34.5 copy.155
  (439 shorter events, 2078.8 us)
Async XLA Ops:
  15.8 7.5 copy-start
  15.8 9.2 copy-start.16
  15.8 9.2 copy-start.17
  15.8 9.2 copy-start.13
  15.8 62.8 %all-to-all-start.2 = ((bf16[4,32,128,64]{2,3,0,1:T(8,128)(2,1)}), bf16[4,32,128,64]{2,3,0,1:T(8,128)(2,1)}, u32[]{:S(2)}, u32[]{:S(2)}) async-start(bf16[4,32,128,64]{2,3,0,1:T(8,128)(2,1)} %convert_bitcast_fusion), calls=%async_computation.2 | async-start | bytes 4194304 | tf_op jit(solution)/shard_map/all_to_all | solution.py:93
  23.7 32.5 copy-start.7
  25.0 31.2 copy-start.9
  25.0 31.1 copy-start.5
  25.0 31.1 copy-start.14
  78.6 16.7 copy-start.19
  78.6 148.4 %all-to-all-start = ((bf16[3,4,32,128,64]{3,4,0,1,2:T(8,128)(2,1)}), bf16[3,4,32,128,64]{3,4,0,1,2:T(8,128)(2,1)}, u32[]{:S(2)}, u32[]{:S(2)}) async-start(bf16[3,4,32,128,64]{3,4,0,1,2:T(8,128)(2,1)} %copy.87), calls=%async_computation | async-start | bytes 12582912 | tf_op jit(solution)/shard_map/all_to_all | solution.py:87
  730.2 1598.7 %all-to-all-start.1 = ((bf16[32,2,16384]{2,1,0:T(2,128)(2,1)}), bf16[32,2,16384]{2,1,0:T(2,128)(2,1)}, u32[]{:S(2)}, u32[]{:S(2)}) async-start(bf16[32,2,16384]{2,1,0:T(2,128)(2,1)} %reshape.405), calls=%async_computation.1 | async-start | bytes 4194304 | tf_op jit(solution)/shard_map/all_to_all | solution.py:89
  2328.9 138.7 %all-to-all-start.3 = ((bf16[32,2,49152]{2,1,0:T(2,128)(2,1)}), bf16[32,2,49152]{2,1,0:T(2,128)(2,1)}, u32[]{:S(2)}, u32[]{:S(2)}) async-start(bf16[32,2,49152]{2,1,0:T(2,128)(2,1)} %reshape.407), calls=%async_computation.3 | async-start | bytes 12582912 | tf_op jit(solution)/shard_map/all_to_all | solution.py:96
  2335.0 1167.8 %all-reduce.4.cloned.1.call-start = ((), (), s32[]{:S(2)}) async-start(), calls=%async_computation.4 | async-start | bytes 134217728 | tf_op jit(solution)/shard_map/psum | solution.py:104
  2344.0 7.1 copy-start.3
  2491.1 18.6 copy-start.1
  2491.1 18.6 copy-start.6
  2491.1 18.6 copy-start.8
  2491.1 18.6 copy-start.10
  2491.1 18.6 copy-start.15
  2533.7 0.7 copy-start.18
  2595.6 30.8 copy-start.12
  2626.4 3.5 copy-start.2
  2626.4 3.5 copy-start.4
  (1 other events, 0.6 us)
Sparse Core Ops, SparseCore 0:
  2533.8 968.9 all-reduce.3
where the time goes:
time: 3570 us; the launch traced here: 3560 us
  matrix products  2050 us (57%)
  waiting for transfers between devices  1050 us (29%)
  local copies, waits for them, and re-layouts  277 us (8%)
  other arithmetic  74.9 us (2%)
  blocking collectives  46.2 us (1%)
  starting transfers between devices  41.4 us (1%)
    psum x1, waiting for transfers between devices, local_block(): lax.psum((d_gamma, d_beta, d_wqkv, d_bqkv, d_wout, d_bout), 'sp')  823 us
    sub x64, matrix products, score_probs(): return jax.nn.softmax(jnp.where(allowed, logits, NEG_BIG), axis=-1)  509 us
    dot_general x32, matrix products, q_step(): jnp.einsum('bhqk,bhqd->bhkd', d_logit, q_part, preferred_element_type=jnp...  481 us
    dot_general x32, matrix products, q_step(): jnp.einsum('bhqk,bhkd->bhqd', d_logit, k_all, preferred_element_type=jnp....  397 us
    dot_general x32, matrix products, q_step(): jnp.einsum('bhqk,bhqd->bhkd', prob_bf, do_part, preferred_element_type=jn...  244 us
    dot_general x32, matrix products, q_step(): jnp.einsum('bhqk,bhkd->bhqd', attn_prob.astype(jnp.bfloat16), v_all, pref...  181 us
    unnamed x50, local copies, waits for them, and re-layouts  155 us
    dot_general x32, matrix products, q_step(): jnp.einsum('bhqd,bhkd->bhqk', do_part, v_all, preferred_element_type=jnp....  130 us
  transfers between devices with their start and end apart: 5, of which 3 were waited for; matrix products, arithmetic and copies ran while one was open for 50% of the time, Pallas kernels for 0%

commit v1 on v0

v1 whole, which is shorter than its diff:
```python
import math
import jax
import jax.numpy as jnp
from jax import lax
from jax.experimental import pallas as pl
from jax.experimental.pallas import tpu as pltpu
from jax.sharding import PartitionSpec as P

LN_EPS = 1e-5
NEG_BIG = -1e30
F32 = jnp.float32
BF16 = jnp.bfloat16
NT = (((1,), (1,)), ((), ()))
NN = (((1,), (0,)), ((), ()))
TILE = 128
WIDTH = 2048
DIM = 64
DEVS = 32
ROWS = 512
BAND = 1024
SEQ = 4096
BQ = 256
BK = 512
LOG2E = 1.4426950408889634


def dot(a, b, dims=NN):
    return lax.dot_general(a, b, dims, preferred_element_type=F32)


def params():
    return pltpu.CompilerParams(vmem_limit_bytes=56 * 2**20)


def low_lanes(shape):
    return lax.broadcasted_iota(jnp.int32, shape, len(shape) - 1) < DIM


def layer_norm(x_rows, gamma_f, beta_f):
    row_mean = jnp.mean(x_rows, axis=-1, keepdims=True)
    centred = x_rows - row_mean
    row_var = jnp.mean(centred * centred, axis=-1, keepdims=True)
    return centred * lax.rsqrt(row_var + LN_EPS) * gamma_f + beta_f


def project_kernel(kind_ref, k_ref, x_ref, w_ref, b_ref, out_ref, buf, sem, *, dims, steps):
    step = pl.program_id(0)
    side = lax.rem(step, 2)

    def copies(at):
        slot = lax.rem(at, 2)
        for i in range(8):
            n = lax.rem(at, 4) * 8 + i
            for half in range(2):
                yield pltpu.make_async_copy(
                    buf.at[slot, i, half],
                    out_ref.at[kind_ref[n], 2 * k_ref[n] + half, lax.div(at, 4)],
                    sem.at[slot],
                )

    @pl.when(step >= 2)
    def _():
        for copy in copies(step - 2):
            copy.wait()

    low = low_lanes((TILE, TILE))
    for pair in range(4):
        cols = slice(pair * TILE, pair * TILE + TILE)
        w_part = w_ref[:, cols] if dims == NN else w_ref[cols, :]
        acc = dot(x_ref[...], w_part, dims) + b_ref[:, cols]
        for half in range(2):
            r0 = acc[half * 256 : half * 256 + TILE]
            r1 = acc[half * 256 + TILE : half * 256 + 256]
            buf[side, 2 * pair, half] = jnp.where(low, r0, pltpu.roll(r1, DIM, 1)).astype(BF16)
            buf[side, 2 * pair + 1, half] = jnp.where(low, pltpu.roll(r0, DIM, 1), r1).astype(BF16)
    for copy in copies(step):
        copy.start()

    @pl.when(step == steps - 1)
    def _():
        for copy in copies(step - 1):
            copy.wait()
        for copy in copies(step):
            copy.wait()


def project(x, w, bias, head_kind, head_k, transposed):
    cols = w.shape[0] if transposed else w.shape[1]
    steps = cols // ROWS
    if transposed:
        w_spec = pl.BlockSpec((ROWS, WIDTH), lambda c, *_: (c, 0))
    else:
        w_spec = pl.BlockSpec((WIDTH, ROWS), lambda c, *_: (0, c))
    body = lambda *refs: project_kernel(*refs, dims=NT if transposed else NN, steps=steps)
    return pl.pallas_call(
        body,
        out_shape=jax.ShapeDtypeStruct((2, DEVS, steps // 4, TILE, TILE), BF16),
        grid_spec=pltpu.PrefetchScalarGridSpec(
            num_scalar_prefetch=2,
            grid=(steps,),
            in_specs=[
                pl.BlockSpec((ROWS, WIDTH), lambda c, *_: (0, 0)),
                w_spec,
                pl.BlockSpec((1, ROWS), lambda c, *_: (0, c)),
            ],
            out_specs=pl.BlockSpec(memory_space=pl.ANY),
            scratch_shapes=[pltpu.VMEM((2, 8, 2, TILE, TILE), BF16), pltpu.SemaphoreType.DMA((2,))],
        ),
        compiler_params=params(),
        cost_estimate=pl.CostEstimate(flops=2 * ROWS * WIDTH * cols, bytes_accessed=WIDTH * cols * 2, transcendentals=0),
        name="project",
    )(head_kind, head_k, x, w, bias)


def unpack_kernel(kind_ref, k_ref, *refs):
    out_ref = refs[8]
    low = low_lanes((TILE, TILE))
    for pair in range(4):
        for half in range(2):
            a = refs[2 * pair][half].astype(F32)
            b = refs[2 * pair + 1][half].astype(F32)
            cols = slice(pair * TILE, pair * TILE + TILE)
            out_ref[half * 256 : half * 256 + TILE, cols] = jnp.where(low, a, pltpu.roll(b, DIM, 1)).astype(BF16)
            out_ref[half * 256 + TILE : half * 256 + 256, cols] = jnp.where(low, pltpu.roll(a, DIM, 1), b).astype(BF16)


def unpack(slots, head_kind, head_k):
    reps = slots.shape[2]
    slots = slots.reshape(2, 16, 2, reps, TILE, TILE)

    def spec(i):
        def index(c, kind_ref, k_ref):
            n = lax.rem(c, 4) * 8 + i
            return kind_ref[n], k_ref[n], 0, lax.div(c, 4), 0, 0

        return pl.BlockSpec((None, None, 2, None, TILE, TILE), index)

    return pl.pallas_call(
        unpack_kernel,
        out_shape=jax.ShapeDtypeStruct((ROWS, reps * WIDTH), BF16),
        grid_spec=pltpu.PrefetchScalarGridSpec(
            num_scalar_prefetch=2,
            grid=(4 * reps,),
            in_specs=[spec(i) for i in range(8)],
            out_specs=pl.BlockSpec((ROWS, ROWS), lambda c, *_: (0, c)),
        ),
        compiler_params=params(),
        cost_estimate=pl.CostEstimate(flops=reps * 2 * 10**9, bytes_accessed=reps * 2**22, transcendentals=0),
        name="unpack",
    )(head_kind, head_k, *([slots] * 8))


def unpack_weights_kernel(kind_ref, k_ref, *refs):
    out_ref = refs[8]
    group = pl.program_id(2)
    low = low_lanes((TILE, TILE))
    for pair in range(4):
        keep_a = kind_ref[group * 8 + 2 * pair] == 0
        keep_b = kind_ref[group * 8 + 2 * pair + 1] == 1

        def rows_step(r, carry, pair=pair, keep_a=keep_a, keep_b=keep_b):
            rows = pl.ds(pl.multiple_of(r * TILE, TILE), TILE)
            a = refs[2 * pair][rows].astype(F32)
            b = refs[2 * pair + 1][rows].astype(F32)
            a = jnp.where(keep_a, a, pltpu.roll(a, DIM, 1))
            b = jnp.where(keep_b, b, pltpu.roll(b, DIM, 1))
            out_ref[rows, pair * TILE : pair * TILE + TILE] = jnp.where(low, a, b)
            return carry

        lax.fori_loop(0, 4, rows_step, 0)


def unpack_weights(gathered, head_kind, head_k):
    def spec(i):
        def index(rh, t, g, kind_ref, k_ref):
            k = k_ref[g * 8 + i]
            fx = lax.div(rh, 2)
            other = lax.rem(k + fx, 2)
            return lax.div(k, 2) * 2 + fx, lax.rem(rh, 2), other * 3 + t, 0, 0

        return pl.BlockSpec((None, None, None, ROWS, TILE), index)

    return pl.pallas_call(
        unpack_weights_kernel,
        out_shape=jax.ShapeDtypeStruct((WIDTH, 3 * WIDTH), F32),
        grid_spec=pltpu.PrefetchScalarGridSpec(
            num_scalar_prefetch=2,
            grid=(4, 3, 4),
            in_specs=[spec(i) for i in range(8)],
            out_specs=pl.BlockSpec((ROWS, ROWS), lambda rh, t, g, *_: (rh, t * 4 + g)),
        ),
        compiler_params=params(),
        cost_estimate=pl.CostEstimate(flops=20 * 10**9, bytes_accessed=100 * 2**20, transcendentals=0),
        name="unpack_weights",
    )(head_kind, head_k, *([gathered] * 8))


def unpack_out(gathered):
    def index(rh, c):
        k = lax.rem(c, 2) * 8 + lax.rem(lax.div(c, 2), 2) * 4 + lax.rem(lax.div(c, 4), 2) * 2 + lax.div(c, 8)
        return k, rh, 3, 0, 0

    def body(in_ref, out_ref):
        out_ref[...] = in_ref[...].reshape(BAND, TILE).astype(F32)

    return pl.pallas_call(
        body,
        out_shape=jax.ShapeDtypeStruct((WIDTH, WIDTH), F32),
        grid=(2, 16),
        in_specs=[pl.BlockSpec((None, None, 2, ROWS, TILE), index)],
        out_specs=pl.BlockSpec((BAND, TILE), lambda rh, c: (rh, c)),
        compiler_params=params(),
        cost_estimate=pl.CostEstimate(flops=5 * 10**9, bytes_accessed=24 * 2**20, transcendentals=0),
        name="unpack_out",
    )(gathered)


def regroup_kernel(f_ref, b_ref, out_ref):
    low = low_lanes((TILE, TILE))
    for r in range(4):
        for t in range(3):
            f = f_ref[r, t].astype(F32)
            b = b_ref[r, t].astype(F32)
            rows = slice(t * TILE, t * TILE + TILE)
            even = jnp.where(low, f, pltpu.roll(b, DIM, 1))
            odd = jnp.where(low, pltpu.roll(f, DIM, 1), b)
            out_ref[rows, r * 256 : r * 256 + TILE] = jnp.transpose(even).astype(BF16)
            out_ref[rows, r * 256 + TILE : r * 256 + 256] = jnp.transpose(odd).astype(BF16)


def regroup(f_slots, b_slots):
    spec = pl.BlockSpec((4, 3, TILE, TILE), lambda r: (r, 0, 0, 0))
    return pl.pallas_call(
        regroup_kernel,
        out_shape=jax.ShapeDtypeStruct((384, 8192), BF16),
        grid=(8,),
        in_specs=[spec, spec],
        out_specs=pl.BlockSpec((384, BAND), lambda r: (0, r)),
        compiler_params=params(),
        cost_estimate=pl.CostEstimate(flops=5 * 10**9, bytes_accessed=12 * 2**20, transcendentals=0),
        name="regroup",
    )(f_slots, b_slots)


def split_pair(rows):
    low = low_lanes(rows.shape)
    zero = jnp.zeros_like(rows)
    return jnp.concatenate([jnp.where(low, rows, zero), jnp.where(low, zero, rows)], axis=0)


def load_rows(ref, index, blocks):
    return ref[pl.ds(index * blocks, blocks)].reshape(blocks * TILE, TILE)


def transpose_into(src_ref, dst):
    def step(r, carry):
        cols = pl.ds(pl.multiple_of(r * TILE, TILE), TILE)
        dst[:, cols] = jnp.transpose(src_ref[r].astype(F32)).astype(BF16)
        return carry

    lax.fori_loop(0, DEVS, step, 0)


def allowed_mask(i, j, banded):
    shape = (BK, 2 * BQ)
    diff = lax.broadcasted_iota(jnp.int32, shape, 0) - (lax.broadcasted_iota(jnp.int32, shape, 1) & (BQ - 1))
    off = i * BQ - j * BK
    keep = diff <= off
    if banded:
        keep = keep & (diff > off - BAND)
    return keep


def forward_kernel(q_ref, k_ref, v_ref, o_ref, lse_ref, v_t, *, banded, scale2):
    transpose_into(v_ref, v_t)

    def q_block(i, carry):
        q_pair = split_pair(load_rows(q_ref, i, 2))

        def scores(j, masked):
            s_t = dot(load_rows(k_ref, j, 4), q_pair, NT)
            return jnp.where(allowed_mask(i, j, banded), s_t, NEG_BIG) if masked else s_t

        def weighted(j, p_t):
            cols = pl.ds(pl.multiple_of(j * BK, BK), BK)
            p_t = p_t.astype(BF16)
            return jnp.concatenate(
                [dot(v_t[0:DIM, cols], p_t[:, 0:BQ]), dot(v_t[DIM:TILE, cols], p_t[:, BQ : 2 * BQ])], axis=1
            )

        last = lax.div(i, 2)
        s_t = scores(last, True)
        m = jnp.max(s_t, axis=0, keepdims=True)
        p_t = jnp.exp2((s_t - m) * scale2)
        state = m, jnp.sum(p_t, axis=0, keepdims=True), weighted(last, p_t)

        def k_block(j, state, masked):
            m, l, acc = state
            s_t = scores(j, masked)
            m_new = jnp.maximum(m, jnp.max(s_t, axis=0, keepdims=True))
            p_t = jnp.exp2((s_t - m_new) * scale2)
            fade = jnp.exp2((m - m_new) * scale2)
            return m_new, l * fade + jnp.sum(p_t, axis=0, keepdims=True), acc * fade + weighted(j, p_t)

        if banded:
            near = jnp.maximum(last - 1, 0)
            state = lax.fori_loop(near, last, lambda j, c: k_block(j, c, False), state)
            state = lax.fori_loop(jnp.maximum(last - 2, 0), near, lambda j, c: k_block(j, c, True), state)
        else:
            state = lax.fori_loop(0, last, lambda j, c: k_block(j, c, False), state)
        m, l, acc = state
        out = acc / l
        out = jnp.transpose(jnp.concatenate([out[:, 0:BQ], out[:, BQ : 2 * BQ]], axis=0))
        o_ref[pl.ds(i * 2, 2)] = out.astype(BF16).reshape(2, TILE, TILE)
        lse_ref[pl.ds(i, 1), :] = m * scale2 + jnp.log2(l)
        return carry

    lax.fori_loop(0, SEQ // BQ, q_block, 0)


def attend_forward(qkv, banded):
    scale2 = LOG2E / math.sqrt(DIM)
    whole = lambda t: pl.BlockSpec((DEVS, None, TILE, TILE), lambda g: (0, t, 0, 0))
    tiles = 42 if banded else 72
    return pl.pallas_call(
        lambda *refs: forward_kernel(*refs, banded=banded, scale2=scale2),
        out_shape=(jax.ShapeDtypeStruct((DEVS, TILE, TILE), BF16), jax.ShapeDtypeStruct((16, 2 * BQ), F32)),
        grid=(1,),
        in_specs=[whole(0), whole(1), whole(2)],
        out_specs=(
            pl.BlockSpec((DEVS, TILE, TILE), lambda g: (0, 0, 0)),
            pl.BlockSpec((16, 2 * BQ), lambda g: (0, 0)),
        ),
        scratch_shapes=[pltpu.VMEM((TILE, SEQ), BF16)],
        compiler_params=params(),
        cost_estimate=pl.CostEstimate(flops=tiles * 5 * 10**8, bytes_accessed=2**22, transcendentals=tiles * 2**18),
        name="forward_band" if banded else "forward_full",
    )(qkv, qkv, qkv)


def backward_kernel(q_ref, k_ref, v_ref, do_ref, o_ref, lse_ref, out_ref, k_t, dq_t, delta, dk_acc, dv_acc, *, banded, scale, scale2):
    transpose_into(k_ref, k_t)

    def prepare(i, carry):
        prod = jnp.transpose(load_rows(do_ref, i, 2).astype(F32) * load_rows(o_ref, i, 2).astype(F32))
        delta[pl.ds(i, 1), :] = jnp.concatenate(
            [jnp.sum(prod[0:DIM], axis=0, keepdims=True), jnp.sum(prod[DIM:TILE], axis=0, keepdims=True)], axis=1
        )
        dq_t[i] = jnp.zeros((TILE, BQ), F32)
        return carry

    lax.fori_loop(0, SEQ // BQ, prepare, 0)

    def k_block(j, carry):
        k_rows = load_rows(k_ref, j, 4)
        v_rows = load_rows(v_ref, j, 4)
        cols = pl.ds(pl.multiple_of(j * BK, BK), BK)
        dk_acc[...] = jnp.zeros_like(dk_acc)
        dv_acc[...] = jnp.zeros_like(dv_acc)

        def q_block(i, carry, masked):
            q_pair = split_pair(load_rows(q_ref, i, 2))
            do_pair = split_pair(load_rows(do_ref, i, 2))
            p_t = jnp.exp2(dot(k_rows, q_pair, NT) * scale2 - lse_ref[pl.ds(i, 1), :])
            if masked:
                p_t = jnp.where(allowed_mask(i, j, banded), p_t, 0.0)
            dp_t = dot(v_rows, do_pair, NT).astype(BF16).astype(F32)
            ds_t = (p_t * (dp_t - delta[pl.ds(i, 1), :]) * scale).astype(BF16)
            dv_acc[...] += dot(p_t.astype(BF16), do_pair)
            dk_acc[...] += dot(ds_t, q_pair)
            dq_t[i, 0:DIM, :] += dot(k_t[0:DIM, cols], ds_t[:, 0:BQ])
            dq_t[i, DIM:TILE, :] += dot(k_t[DIM:TILE, cols], ds_t[:, BQ : 2 * BQ])
            return carry

        first = 2 * j
        lax.fori_loop(first, first + 2, lambda i, c: q_block(i, c, True), 0)
        if banded:
            edge = jnp.minimum(first + 4, 16)
            lax.fori_loop(first + 2, edge, lambda i, c: q_block(i, c, False), 0)
            lax.fori_loop(edge, jnp.minimum(first + 6, 16), lambda i, c: q_block(i, c, True), 0)
        else:
            lax.fori_loop(first + 2, 16, lambda i, c: q_block(i, c, False), 0)
        out_ref[pl.ds(j * 4, 4), 1] = dk_acc[...].astype(BF16).reshape(4, TILE, TILE)
        out_ref[pl.ds(j * 4, 4), 2] = dv_acc[...].astype(BF16).reshape(4, TILE, TILE)
        return carry

    lax.fori_loop(0, SEQ // BK, k_block, 0)

    def finish(i, carry):
        out_ref[pl.ds(i * 2, 2), 0] = jnp.transpose(dq_t[i]).astype(BF16).reshape(2, TILE, TILE)
        return carry

    lax.fori_loop(0, SEQ // BQ, finish, 0)


def attend_backward(qkv, d_out, out, lse, banded):
    scale = 1.0 / math.sqrt(DIM)
    whole = lambda t: pl.BlockSpec((DEVS, None, TILE, TILE), lambda g: (0, t, 0, 0))
    flat = pl.BlockSpec((DEVS, TILE, TILE), lambda g: (0, 0, 0))
    of_kind = pl.BlockSpec((None, DEVS, TILE, TILE), lambda g: (1 if banded else 0, 0, 0, 0))
    tiles = 42 if banded else 72
    return pl.pallas_call(
        lambda *refs: backward_kernel(*refs, banded=banded, scale=scale, scale2=scale * LOG2E),
        out_shape=jax.ShapeDtypeStruct((DEVS, 3, TILE, TILE), BF16),
        grid=(1,),
        in_specs=[whole(0), whole(1), whole(2), of_kind, flat, pl.BlockSpec((16, 2 * BQ), lambda g: (0, 0))],
        out_specs=pl.BlockSpec((DEVS, 3, TILE, TILE), lambda g: (0, 0, 0, 0)),
        scratch_shapes=[
            pltpu.VMEM((TILE, SEQ), BF16),
            pltpu.VMEM((16, TILE, BQ), F32),
            pltpu.VMEM((16, 2 * BQ), F32),
            pltpu.VMEM((BK, TILE), F32),
            pltpu.VMEM((BK, TILE), F32),
        ],
        compiler_params=params(),
        cost_estimate=pl.CostEstimate(flops=tiles * 10**9, bytes_accessed=2**23, transcendentals=tiles * 2**18),
        name="backward_band" if banded else "backward_full",
    )(qkv, qkv, qkv, d_out, out, lse)


def exchange(slots):
    return lax.all_to_all(slots, "sp", 0, 0, tiled=True)


def solution(mesh):
    tok_spec = P(None, "sp", None)
    pair_swap = [(i, i ^ 1) for i in range(DEVS)]
    x_swap = [(i, i ^ 2) for i in range(DEVS)]
    same_xc = [list(range(c, DEVS, 4)) for c in range(4)]

    def layer(x, d_y, ln_gamma, ln_beta, w_qkv, b_qkv, w_out, b_out, head_kind):
        half = lax.rem(lax.axis_index("sp"), 2)
        x_bit = lax.rem(lax.div(lax.axis_index("sp"), 2), 2)
        head = jnp.arange(DEVS)
        banded_before = jnp.sum(jnp.where(head[None, :] < head[:, None], head_kind[None, :], 0), axis=1)
        head_k = jnp.where(head_kind == 1, banded_before, head - banded_before).astype(jnp.int32)

        x_f = x.astype(F32)
        h_f, ln_pull = jax.vjp(layer_norm, x_f, ln_gamma.astype(F32), ln_beta.astype(F32))
        h_norm = h_f.astype(BF16)
        d_y_rows = d_y.reshape(ROWS, WIDTH)

        def trade(array, bit, width, axis, flip):
            keep = lax.dynamic_slice_in_dim(array, bit * width, width, axis)
            take = lax.ppermute(lax.dynamic_slice_in_dim(array, width - bit * width, width, axis), "sp", flip)
            return jnp.where(bit == 0, jnp.stack([keep, take]), jnp.stack([take, keep]))

        h_part = trade(h_norm, half, 2, 0, pair_swap)
        h_part = trade(h_part, x_bit, BAND, 3, x_swap)
        h_all = lax.all_gather(h_part, "sp", axis_index_groups=same_xc).reshape(2 * SEQ, BAND)
        qkv_slots = project(h_norm.reshape(ROWS, WIDTH), w_qkv, b_qkv.astype(F32).reshape(1, 3 * WIDTH), head_kind, head_k, False)
        d_attn_slots = project(d_y_rows, w_out, jnp.zeros((1, WIDTH), F32), head_kind, head_k, True)
        qkv_full = exchange(qkv_slots[0])
        qkv_band = exchange(qkv_slots[1])
        qkv_full, d_attn_slots = lax.optimization_barrier((qkv_full, d_attn_slots))
        d_attn = lax.all_to_all(d_attn_slots.reshape(2, DEVS, TILE, TILE), "sp", 1, 1, tiled=True)
        attn_full, lse_full = attend_forward(qkv_full, False)
        o_full = exchange(attn_full)
        qkv_band, attn_full = lax.optimization_barrier((qkv_band, attn_full))
        attn_band, lse_band = attend_forward(qkv_band, True)
        o_band = exchange(attn_band)
        attn_slots = jnp.stack([o_full, o_band])[:, :, None]
        attn_tok = unpack(attn_slots, head_kind, head_k)
        proj_out = dot(attn_tok, w_out).reshape(4, TILE, WIDTH)
        y_out = (x_f + proj_out + b_out.astype(F32)).astype(BF16)
        d_wout = dot(attn_tok, d_y_rows, (((0,), (0,)), ((), ())))

        def halve(part, step):
            bit = lax.rem(lax.div(lax.axis_index("sp"), 2**step), 2)
            axis = 1 if step else 0
            width = part.shape[axis] // 2
            keep = lax.dynamic_slice_in_dim(part, bit * width, width, axis)
            give = lax.dynamic_slice_in_dim(part, width - bit * width, width, axis).astype(BF16)
            take = lax.ppermute(give, "sp", [(i, i ^ 2**step) for i in range(DEVS)])
            return keep + take.astype(F32)

        for step in range(5):
            d_wout = halve(d_wout, step)
        d_qkv_full = attend_backward(qkv_full, d_attn, attn_full, lse_full, False)
        p_full = lax.ppermute(d_qkv_full, "sp", x_swap)
        g_full = exchange(d_qkv_full)
        lse_band, d_qkv_full = lax.optimization_barrier((lse_band, d_qkv_full))
        d_qkv_band = attend_backward(qkv_band, d_attn, attn_band, lse_band, True)
        p_band = lax.ppermute(d_qkv_band, "sp", x_swap)
        g_band = exchange(d_qkv_band)
        d_qkv_slots = jnp.stack([g_full, g_band])

        d_own = regroup(d_qkv_full, d_qkv_band)
        dw_own = dot(d_own, h_all)
        d_part = regroup(p_full, p_band)
        dw_part = dot(d_part, h_all)
        dw_all = jnp.stack([dw_own, dw_part])
        dw_mine = lax.dynamic_slice_in_dim(dw_all, half * ROWS, ROWS, 2)
        dw_other = lax.dynamic_slice_in_dim(dw_all, ROWS - half * ROWS, ROWS, 2)
        dw_other = lax.ppermute(dw_other, "sp", pair_swap)
        dw_sum = (dw_mine + dw_other).astype(BF16).reshape(6, TILE, ROWS).transpose(0, 2, 1)
        shares = jnp.concatenate([dw_sum, d_wout.astype(BF16).reshape(2, ROWS, TILE)])
        shares = lax.all_gather(shares, "sp").reshape(16, 2, 8, ROWS, TILE)
        d_wout = unpack_out(shares)
        d_wqkv = unpack_weights(shares, head_kind, head_k)

        d_qkv_tok = unpack(d_qkv_slots, head_kind, head_k)
        d_bqkv = jnp.sum(d_qkv_tok, axis=0, dtype=F32)
        d_h = dot(d_qkv_tok, w_qkv, NT).astype(BF16).astype(F32).reshape(4, TILE, WIDTH)
        d_x_ln, d_gamma, d_beta = ln_pull(d_h)
        d_x = (d_y.astype(F32) + d_x_ln).astype(BF16)
        d_bout = jnp.sum(d_y_rows, axis=0, dtype=F32)
        d_gamma, d_beta, d_bqkv, d_bout = lax.psum((d_gamma, d_beta, d_bqkv, d_bout), "sp")
        return y_out, d_x, d_gamma, d_beta, d_wqkv, d_bqkv, d_wout, d_bout

    return jax.shard_map(layer, mesh=mesh, in_specs=(tok_spec, tok_spec, P(), P(), P(), P(), P(), P(), P()), out_specs=(tok_spec, tok_spec, P(), P(), P(), P(), P(), P()), check_vma=False)
```

time: 3570 us -> 1340 us (0.38)
  matrix products: 2050 us -> 60 us
  waiting for transfers between devices: 1050 us -> 497 us
  Pallas kernels: 0 us -> 403 us
  local copies, waits for them, and re-layouts: 277 us -> 34.6 us
  blocking collectives: 46.2 us -> 240 us
    dot_general x166 -> x5, matrix products: 1540 us -> 60 us  [dot(): return lax.dot_general(a, b, dims, preferred_element_type=F32)]
    psum x1 -> x0, waiting for transfers between devices: 823 us -> none  [local_block(): lax.psum((d_gamma, d_beta, d_wqkv, d_bqkv, d_wout, d_bout), 'sp')]
    sub x64 -> x0, matrix products: 509 us -> none  [score_probs(): return jax.nn.softmax(jnp.where(allowed, logits, NEG_BIG), axis=-1)]
    pallas_call x0 -> x12, Pallas kernels: none -> 403 us  [the longest x2 120 us: attend_backward(): pl.pallas_call(lambda *refs: backward_kernel(*refs, banded=banded, scale=...]
    all_to_all x0 -> x2, blocking collectives: none -> 199 us  [exchange(): return lax.all_to_all(slots, 'sp', 0, 0, tiled=True)]
    ppermute x0 -> x10, waiting for transfers between devices: none -> 179 us  [the longest x1 66.2 us: layer(): p_band = lax.ppermute(d_qkv_band, 'sp', x_swap)]
    unnamed x50 -> x60, local copies, waits for them, and re-layouts: 155 us -> 16.2 us
    all_to_all x4 -> x5, waiting for transfers between devices: 232 us -> 319 us  [the longest x4 263 us: exchange(): return lax.all_to_all(slots, 'sp', 0, 0, tiled=True)]
  transfers between devices with their start and end apart: 5 -> 17, of which waited for: 3 -> 9; matrix products, arithmetic and copies ran while one was open for 50% -> 8% of each run, Pallas kernels for 0% -> 20%
where the time goes in v1:
time: 1340 us; the launch traced here: 1320 us
  waiting for transfers between devices  497 us (37%)
  Pallas kernels  403 us (30%)
  blocking collectives  240 us (18%)
  matrix products  60 us (4%)
  other arithmetic  44.3 us (3%)
  local copies, waits for them, and re-layouts  34.6 us (3%)
  starting transfers between devices  30.1 us (2%)
  between operations  14.8 us (1%)
    all_to_all x4, waiting for transfers between devices, exchange(): return lax.all_to_all(slots, 'sp', 0, 0, tiled=True)  263 us
    all_to_all x2, blocking collectives, exchange(): return lax.all_to_all(slots, 'sp', 0, 0, tiled=True)  199 us
    pallas_call x2, Pallas kernels, attend_backward(): pl.pallas_call(lambda *refs: backward_kernel(*refs, banded=banded, scale=...  120 us
    pallas_call x2, Pallas kernels, attend_forward(): pl.pallas_call(lambda *refs: forward_kernel(*refs, banded=banded, scale2=...  94.5 us
    pallas_call x1, Pallas kernels, unpack_weights(): pl.pallas_call(unpack_weights_kernel, out_shape=jax.ShapeDtypeStruct((WID...  86.1 us
    ppermute x1, waiting for transfers between devices, layer(): p_band = lax.ppermute(d_qkv_band, 'sp', x_swap)  66.2 us
    ppermute x5, waiting for transfers between devices, halve(): take = lax.ppermute(give, 'sp', [(i, i ^ 2 ** step) for i in range(DEVS)])  60.3 us
    dot_general x5, matrix products, dot(): return lax.dot_general(a, b, dims, preferred_element_type=F32)  60 us
  transfers between devices with their start and end apart: 17, of which 9 were waited for; matrix products, arithmetic and copies ran while one was open for 8% of the time, Pallas kernels for 20%

profile of v1, /device:TPU:0, one launch (start us, length us, event | category | flops | bytes accessed | tf_op | source)
XLA Modules:
  0.0 1324.1 jit_solution(16650796825917804880)
XLA Ops:
  15.1 33.1 %project.2 = bf16[2,32,3,128,128]{4,3,2,1,0:T(8,128)(2,1)} custom-call(s32[32]{0:T(128)} %kind_ref.5, s32[32]{0:T(128)} %compare_select_fusion.refs_1_.k_ref, bf16[512,2048]{1,0:T(8,128)(2,1)} %bitcast.56, bf16[2048,6144]{1,0:T(8,128)(2,1)} %refs_3_.2, f32[1,6144]{1,0:T(1,128)} %bitcast.67), custom_call_target="tpu_custom_call" | custom-call | flops 12884901888 | bytes 25165824 | tf_op jit(solution)/shard_map/project/pallas_call | solution.py:95
  65.1 69.9 %all-to-all-done.refs_0_.refs_1_.refs_2_ = bf16[32,3,128,128]{3,2,1,0:T(8,128)(2,1)} async-done(((bf16[32,3,128,128]{3,2,1,0:T(8,128)(2,1)}), bf16[32,3,128,128]{3,2,1,0:T(8,128)(2,1)}, u32[]{:S(2)}, u32[]{:S(2)}) %all-to-all-start) | async-done | bytes 3145760 | tf_op jit(solution)/shard_map/all_to_all | solution.py:422
  141.7 52.3 %collective-permute-done.1 = bf16[2,2,128,1024]{3,2,1,0:T(8,128)(2,1)S(1)} collective-permute-done((bf16[2,2,128,1024]{3,2,1,0:T(8,128)(2,1)S(1)}, bf16[2,2,128,1024]{3,2,1,0:T(8,128)(2,1)S(1)}, u32[]{:S(2)}, u32[]{:S(2)}) %collective-permute-start.1) | collective-permute-done | bytes 1048608 | tf_op jit(solution)/shard_map/ppermute | solution.py:445
  196.2 13.5 %project.3 = bf16[2,32,1,128,128]{4,3,2,1,0:T(8,128)(2,1)} custom-call(s32[32]{0:T(128)} %kind_ref.5, s32[32]{0:T(128)} %compare_select_fusion.refs_1_.k_ref, bf16[512,2048]{1,0:T(8,128)(2,1)} %bitcast.62, bf16[2048,2048]{1,0:T(8,128)(2,1)} %refs_3_.3, f32[1,2048]{1,0:T(1,128)} %broadcast_in_dim.31.refs_4_), custom_call_target="tpu_custom_call" | custom-call | flops 4294967296 | bytes 8388608 | tf_op jit(solution)/shard_map/project/pallas_call | solution.py:95
  209.7 56.6 %forward_full.1 = (bf16[32,128,128]{2,1,0:T(8,128)(2,1)}, f32[16,512]{1,0:T(8,128)}) custom-call(bf16[32,3,128,128]{3,2,1,0:T(8,128)(2,1)} %all-to-all-done.refs_0_.refs_1_.refs_2_, bf16[32,3,128,128]{3,2,1,0:T(8,128)(2,1)} %all-to-all-done.refs_0_.refs_1_.refs_2_, bf16[32,3,128,128]{3,2,1,0:T(8,128)(2,1)} %all-to-all-done.refs_0_.refs_1_.refs_2_), custom_call_target="tpu_custom_call" | custom-call | flops 35999997952 | bytes 4194304 | tf_op jit(solution)/shard_map/forward_full/pallas_call | solution.py:325
  266.3 37.9 %forward_band.1 = (bf16[32,128,128]{2,1,0:T(8,128)(2,1)}, f32[16,512]{1,0:T(8,128)}) custom-call(bf16[32,3,128,128]{3,2,1,0:T(8,128)(2,1)} %all-to-all-done.2.refs_0_.refs_1_.refs_2_, bf16[32,3,128,128]{3,2,1,0:T(8,128)(2,1)} %all-to-all-done.2.refs_0_.refs_1_.refs_2_, bf16[32,3,128,128]{3,2,1,0:T(8,128)(2,1)} %all-to-all-done.2.refs_0_.refs_1_.refs_2_), custom_call_target="tpu_custom_call" | custom-call | flops 20999999488 | bytes 4194304 | tf_op jit(solution)/shard_map/forward_band/pallas_call | solution.py:325
  304.2 61.9 %all_to_all.35 = bf16[32,128,128]{2,1,0:T(8,128)(2,1)S(1)} all-to-all(bf16[32,128,128]{2,1,0:T(8,128)(2,1)} %get-tuple-element.21.refs_4_), channel_id=1, replica_groups=mesh['sp'=32] {'sp'}, dimensions={0} | all-to-all | bytes 2097152 | tf_op jit(solution)/shard_map/all_to_all | solution.py:422
  372.1 55.9 %all-to-all-done.1 = bf16[32,128,128]{2,1,0:T(8,128)(2,1)S(1)} async-done(((bf16[32,128,128]{2,1,0:T(8,128)(2,1)}), bf16[32,128,128]{2,1,0:T(8,128)(2,1)S(1)}, u32[]{:S(2)}, u32[]{:S(2)}) %all-to-all-start.1) | async-done | bytes 1048608 | tf_op jit(solution)/shard_map/all_to_all | solution.py:422
  455.3 56.1 %all-to-all-done.4 = bf16[2,32,128,128]{3,2,0,1:T(8,128)(2,1)S(1)} async-done(((bf16[2,32,128,128]{3,2,0,1:T(8,128)(2,1)}), bf16[2,32,128,128]{3,2,0,1:T(8,128)(2,1)S(1)}, u32[]{:S(2)}, u32[]{:S(2)}) %all-to-all-start.4) | async-done | bytes 2097184 | tf_op jit(solution)/shard_map/all_to_all | solution.py:456
  512.8 69.9 %backward_full.1.f_ref = bf16[32,3,128,128]{3,2,1,0:T(8,128)(2,1)} custom-call(bf16[32,3,128,128]{3,2,1,0:T(8,128)(2,1)} %all-to-all-done.refs_0_.refs_1_.refs_2_, bf16[32,3,128,128]{3,2,1,0:T(8,128)(2,1)} %all-to-all-done.refs_0_.refs_1_.refs_2_, bf16[32,3,128,128]{3,2,1,0:T(8,128)(2,1)} %all-to-all-done.refs_0_.refs_1_.refs_2_, ...), custom_call_target="tpu_custom_call" | custom-call | flops 71999995904 | bytes 8388608 | tf_op jit(solution)/shard_map/backward_full/pallas_call | solution.py:402
  584.3 49.7 %backward_band.1.b_ref = bf16[32,3,128,128]{3,2,1,0:T(8,128)(2,1)} custom-call(bf16[32,3,128,128]{3,2,1,0:T(8,128)(2,1)} %all-to-all-done.2.refs_0_.refs_1_.refs_2_, bf16[32,3,128,128]{3,2,1,0:T(8,128)(2,1)} %all-to-all-done.2.refs_0_.refs_1_.refs_2_, bf16[32,3,128,128]{3,2,1,0:T(8,128)(2,1)} %all-to-all-done.2.refs_0_.refs_1_.refs_2_, ...), custom_call_target="tpu_custom_call" | custom-call | flops 41999998976 | bytes 8388608 | tf_op jit(solution)/shard_map/backward_band/pallas_call | solution.py:402
  655.3 66.2 %collective-permute-done.3.b_ref = bf16[32,3,128,128]{3,2,1,0:T(8,128)(2,1)} collective-permute-done((bf16[32,3,128,128]{3,2,1,0:T(8,128)(2,1)}, bf16[32,3,128,128]{3,2,1,0:T(8,128)(2,1)}, u32[]{:S(2)}, u32[]{:S(2)}) %collective-permute-start.3) | collective-permute-done | bytes 3145760 | tf_op jit(solution)/shard_map/ppermute | solution.py:484
  730.8 34.7 %collective-permute-done.6 = bf16[1024,1024]{1,0:T(8,128)(2,1)} collective-permute-done((bf16[1024,1024]{1,0:T(8,128)(2,1)S(1)}, bf16[1024,1024]{1,0:T(8,128)(2,1)}, u32[]{:S(2)}, u32[]{:S(2)}) %collective-permute-start.6) | collective-permute-done | bytes 2097184 | tf_op jit(solution)/shard_map/ppermute | solution.py:474
  772.9 12.2 convolution_bitcast_fusion.1
  798.8 12.9 collective-permute-done.8
  813.2 12.7 collective-permute-done.9
  829.5 136.7 %all_to_all.36 = bf16[32,3,128,128]{3,2,1,0:T(8,128)(2,1)S(1)} all-to-all(bf16[32,3,128,128]{3,2,1,0:T(8,128)(2,1)} %backward_band.1.b_ref), channel_id=1, replica_groups=mesh['sp'=32] {'sp'}, dimensions={0} | all-to-all | bytes 6291456 | tf_op jit(solution)/shard_map/all_to_all | solution.py:422
  971.3 10.6 fusion.22
  981.9 136.7 %all-to-all-done.5 = bf16[32,3,128,128]{3,2,1,0:T(8,128)(2,1)} async-done(((bf16[32,3,128,128]{3,2,1,0:T(8,128)(2,1)}), bf16[32,3,128,128]{3,2,1,0:T(8,128)(2,1)}, u32[]{:S(2)}, u32[]{:S(2)}) %all-to-all-start.5) | async-done | bytes 3145760 | tf_op jit(solution)/shard_map/all_to_all | solution.py:422
  1123.7 11.3 unpack.3
  1135.0 21.2 %fusion.21 = (f32[2048]{0:T(1024)S(1)}, f32[512,2048]{1,0:T(8,128)}) fusion(bf16[512,6144]{1,0:T(8,128)(2,1)} %unpack.3, bf16[2048,6144]{1,0:T(8,128)(2,1)} %refs_3_.2), kind=kOutput, calls=%fused_computation.63 | convolution fusion | flops 12888045568 | bytes 35659776 | tf_op jit(solution)/shard_map/dot_general | solution.py:28
  1168.9 41.7 %all-reduce = (f32[2048]{0:T(1024)}, f32[2048]{0:T(1024)}, f32[6144]{0:T(1024)}, f32[2048]{0:T(1024)}) all-reduce(f32[2048]{0:T(1024)S(1)} %get-tuple-element.28, f32[2048]{0:T(1024)S(1)} %get-tuple-element.43, f32[6144]{0:T(1024)S(1)} %convert_reduce_fusion, f32[2048]{0:T(1024)S(1)} %get-tuple-element.40), channel_id=1, replica_groups=mesh['sp'=32] {'sp'}, use_global_device_ids=true, to_apply=%region_6.7 | all-reduce | flops 12288 | bytes 98304 | tf_op jit(solution)/shard_map/psum | solution.py:508
  1210.6 86.1 %unpack_weights.1 = f32[2048,6144]{1,0:T(8,128)} custom-call(s32[32]{0:T(128)} %kind_ref.5, s32[32]{0:T(128)} %compare_select_fusion.refs_1_.k_ref, bf16[16,2,8,512,128]{4,3,2,1,0:T(8,128)(2,1)} %bitcast.42, bf16[16,2,8,512,128]{4,3,2,1,0:T(8,128)(2,1)} %bitcast.43, bf16[16,2,8,512,128]{4,3,2,1,0:T(8,128)(2,1)} %bitcast.44, ...), custom_call_target="tpu_custom_call" | custom-call | flops 20000000000 | bytes 104857600 | tf_op jit(solution)/shard_map/unpack_weights/pallas_call | solution.py:183
  1296.7 20.4 %unpack_out.1 = f32[2048,2048]{1,0:T(8,128)} custom-call(bf16[16,2,8,512,128]{4,3,2,1,0:T(8,128)(2,1)} %bitcast.50), custom_call_target="tpu_custom_call" | custom-call | flops 5000000000 | bytes 25165824 | tf_op jit(solution)/shard_map/unpack_out/pallas_call | solution.py:206
  (134 shorter events, 149.3 us)
Async XLA Ops:
  56.3 7.5 copy-start.7
  56.3 78.8 %all-to-all-start = ((bf16[32,3,128,128]{3,2,1,0:T(8,128)(2,1)}), bf16[32,3,128,128]{3,2,1,0:T(8,128)(2,1)}, u32[]{:S(2)}, u32[]{:S(2)}) async-start(bf16[32,3,128,128]{3,2,1,0:T(8,128)(2,1)} %get-tuple-element.34), calls=%async_computation | async-start | bytes 6291456 | tf_op jit(solution)/shard_map/all_to_all | solution.py:422
  65.0 74.3 %collective-permute-start = (bf16[2,128,2048]{2,1,0:T(8,128)(2,1)}, bf16[2,128,2048]{2,1,0:T(8,128)(2,1)S(1)}, u32[]{:S(2)}, u32[]{:S(2)}) collective-permute-start(bf16[2,128,2048]{2,1,0:T(8,128)(2,1)} %get-tuple-element.39), channel_id=1, source_target_pairs={{0,1},{1,0},{2,3},{3,2},{4,5},{5,4},{6,7},{7,6},{8,9},{9,8},{10,11... | collective-permute-start | bytes 3145736 | tf_op jit(solution)/shard_map/ppermute | solution.py:445
  135.1 131.2 %all-to-all-start.2 = ((bf16[32,3,128,128]{3,2,1,0:T(8,128)(2,1)}), bf16[32,3,128,128]{3,2,1,0:T(8,128)(2,1)}, u32[]{:S(2)}, u32[]{:S(2)}) async-start(bf16[32,3,128,128]{3,2,1,0:T(8,128)(2,1)} %get-tuple-element.35), calls=%async_computation.2 | async-start | bytes 6291456 | tf_op jit(solution)/shard_map/all_to_all | solution.py:422
  139.2 633.6 %all-gather.4.cloned.1.call-start = ((), (), s32[]{:S(2)}) async-start(), calls=%async_computation.7 | async-start | bytes 18874368 | tf_op jit(solution)/shard_map/all_gather | solution.py:450
  139.9 54.1 %collective-permute-start.1 = (bf16[2,2,128,1024]{3,2,1,0:T(8,128)(2,1)S(1)}, bf16[2,2,128,1024]{3,2,1,0:T(8,128)(2,1)S(1)}, u32[]{:S(2)}, u32[]{:S(2)}) collective-permute-start(bf16[2,2,128,1024]{3,2,1,0:T(8,128)(2,1)S(1)} %get-tuple-element.37), channel_id=1, source_target_pairs={{0,2},{1,3},{2,0},{3,1},{4,6},{5,7},{6,4},{7,5},{8,10},{9,11},{10,... | collective-permute-start | bytes 3145736 | tf_op jit(solution)/shard_map/ppermute | solution.py:445
  366.1 61.8 %all-to-all-start.1 = ((bf16[32,128,128]{2,1,0:T(8,128)(2,1)}), bf16[32,128,128]{2,1,0:T(8,128)(2,1)S(1)}, u32[]{:S(2)}, u32[]{:S(2)}) async-start(bf16[32,128,128]{2,1,0:T(8,128)(2,1)} %get-tuple-element.23.refs_4_), calls=%async_computation.1 | async-start | bytes 2097152 | tf_op jit(solution)/shard_map/all_to_all | solution.py:422
  428.9 82.4 %all-to-all-start.4 = ((bf16[2,32,128,128]{3,2,0,1:T(8,128)(2,1)}), bf16[2,32,128,128]{3,2,0,1:T(8,128)(2,1)S(1)}, u32[]{:S(2)}, u32[]{:S(2)}) async-start(bf16[2,32,128,128]{3,2,0,1:T(8,128)(2,1)} %copy.22), calls=%async_computation.4 | async-start | bytes 4194304 | tf_op jit(solution)/shard_map/all_to_all | solution.py:456
  431.7 778.9 %all-gather.6.cloned.1.call-start = ((), (), s32[]{:S(2)}) async-start(), calls=%async_computation.8 | async-start | bytes 34603008 | tf_op jit(solution)/shard_map/all_gather | solution.py:498
  446.2 6.2 copy-start.6
  455.0 179.4 %collective-permute-start.5 = (bf16[1024,2048]{1,0:T(8,128)(2,1)}, bf16[1024,2048]{1,0:T(8,128)(2,1)}, u32[]{:S(2)}, u32[]{:S(2)}) collective-permute-start(bf16[1024,2048]{1,0:T(8,128)(2,1)} %dynamic-slice_convert_fusion), channel_id=1, source_target_pairs={{0,1},{1,0},{2,3},{3,2},{4,5},{5,4},{6,7},{7,6},{8,9},{9,8},{10,11... | collective-permute-start | bytes 12582920 | tf_op jit(solution)/shard_map/ppermute | solution.py:474
  582.7 72.5 %collective-permute-start.2 = (bf16[32,3,128,128]{3,2,1,0:T(8,128)(2,1)}, bf16[32,3,128,128]{3,2,1,0:T(8,128)(2,1)}, u32[]{:S(2)}, u32[]{:S(2)}) collective-permute-start(bf16[32,3,128,128]{3,2,1,0:T(8,128)(2,1)} %backward_full.1.f_ref), channel_id=1, source_target_pairs={{0,2},{1,3},{2,0},{3,1},{4,6},{5,7},{6,4},{7,5},{8,10},{9,11},{10,... | collective-permute-start | bytes 9437192 | tf_op jit(solution)/shard_map/ppermute | solution.py:480
  634.0 87.4 %collective-permute-start.3 = (bf16[32,3,128,128]{3,2,1,0:T(8,128)(2,1)}, bf16[32,3,128,128]{3,2,1,0:T(8,128)(2,1)}, u32[]{:S(2)}, u32[]{:S(2)}) collective-permute-start(bf16[32,3,128,128]{3,2,1,0:T(8,128)(2,1)} %backward_band.1.b_ref), channel_id=1, source_target_pairs={{0,2},{1,3},{2,0},{3,1},{4,6},{5,7},{6,4},{7,5},{8,10},{9,11},{10,... | collective-permute-start | bytes 9437192 | tf_op jit(solution)/shard_map/ppermute | solution.py:484
  644.1 121.4 %collective-permute-start.6 = (bf16[1024,1024]{1,0:T(8,128)(2,1)S(1)}, bf16[1024,1024]{1,0:T(8,128)(2,1)}, u32[]{:S(2)}, u32[]{:S(2)}) collective-permute-start(bf16[1024,1024]{1,0:T(8,128)(2,1)S(1)} %dynamic-slice_convert_fusion.1), channel_id=1, source_target_pairs={{0,2},{1,3},{2,0},{3,1},{4,6},{5,7},{6,4},{7,5},{8,10},{9,11},{10,... | collective-permute-start | bytes 6291464 | tf_op jit(solution)/shard_map/ppermute | solution.py:474
  771.2 25.0 %collective-permute-start.7 = (bf16[1024,512]{1,0:T(8,128)(2,1)S(1)}, bf16[1024,512]{1,0:T(8,128)(2,1)S(1)}, u32[]{:S(2)}, u32[]{:S(2)}) collective-permute-start(bf16[1024,512]{1,0:T(8,128)(2,1)S(1)} %dynamic-slice_convert_fusion.2), channel_id=1, source_target_pairs={{0,4},{1,5},{2,6},{3,7},{4,0},{5,1},{6,2},{7,3},{8,12},{9,13},{10,... | collective-permute-start | bytes 3145736 | tf_op jit(solution)/shard_map/ppermute | solution.py:474
  772.9 12.3 copy-start.27
  785.2 9.7 copy-start.8
  796.2 29.7 %collective-permute-start.4 = (f32[2,384,512]{2,1,0:T(8,128)}, f32[2,384,512]{2,1,0:T(8,128)}, u32[]{:S(2)}, u32[]{:S(2)}) collective-permute-start(f32[2,384,512]{2,1,0:T(8,128)} %fusion.16), channel_id=1, source_target_pairs={{0,1},{1,0},{2,3},{3,2},{4,5},{5,4},{6,7},{7,6},{8,9},{9,8},{10,11... | collective-permute-start | bytes 4718600 | tf_op jit(solution)/shard_map/ppermute | solution.py:495
  798.7 13.0 collective-permute-start.8
  812.9 12.9 collective-permute-start.9
  966.3 152.3 %all-to-all-start.5 = ((bf16[32,3,128,128]{3,2,1,0:T(8,128)(2,1)}), bf16[32,3,128,128]{3,2,1,0:T(8,128)(2,1)}, u32[]{:S(2)}, u32[]{:S(2)}) async-start(bf16[32,3,128,128]{3,2,1,0:T(8,128)(2,1)} %backward_full.1.f_ref), calls=%async_computation.5 | async-start | bytes 6291456 | tf_op jit(solution)/shard_map/all_to_all | solution.py:422
  1135.0 21.3 %copy-start.1 = (bf16[4,128,2048]{2,1,0:T(8,128)(2,1)S(1)}, bf16[4,128,2048]{2,1,0:T(8,128)(2,1)}, u32[]{:S(2)}) copy-start(bf16[4,128,2048]{2,1,0:T(8,128)(2,1)} %param.9) | copy-start | bytes 6291460
  1135.0 21.3 %copy-start.15 = (f32[2048]{0:T(1024)S(1)}, f32[2048]{0:T(1024)}, u32[]{:S(2)}) copy-start(f32[2048]{0:T(1024)} %copy-done.14) | copy-start | bytes 24580
  1135.0 21.3 %copy-start.17 = (f32[4,128]{1,0:T(4,128)S(1)}, f32[4,128]{1,0:T(4,128)}, u32[]{:S(2)}) copy-start(f32[4,128]{1,0:T(4,128)} %copy-done.16) | copy-start | bytes 6148
  (23 other events, 84.4 us)
Sparse Core Ops, SparseCore 0:
  195.7 315.1 all-gather.3
  829.6 306.4 all-gather.5

commit v2 on v1

--- a/solution.py
+++ b/solution.py
@@ -153,66 +153,64 @@
 def unpack_weights_kernel(kind_ref, k_ref, *refs):
     out_ref = refs[8]
     group = pl.program_id(2)
-    low = low_lanes((TILE, TILE))
+    low = low_lanes((ROWS, TILE))
     for pair in range(4):
         keep_a = kind_ref[group * 8 + 2 * pair] == 0
         keep_b = kind_ref[group * 8 + 2 * pair + 1] == 1
 
         def rows_step(r, carry, pair=pair, keep_a=keep_a, keep_b=keep_b):
-            rows = pl.ds(pl.multiple_of(r * TILE, TILE), TILE)
-            a = refs[2 * pair][rows].astype(F32)
-            b = refs[2 * pair + 1][rows].astype(F32)
+            a = refs[2 * pair][r].astype(F32)
+            b = refs[2 * pair + 1][r].astype(F32)
             a = jnp.where(keep_a, a, pltpu.roll(a, DIM, 1))
             b = jnp.where(keep_b, b, pltpu.roll(b, DIM, 1))
-            out_ref[rows, pair * TILE : pair * TILE + TILE] = jnp.where(low, a, b)
+            out_ref[r, :, pair * TILE : pair * TILE + TILE] = jnp.where(low, a, b)
             return carry
 
-        lax.fori_loop(0, 4, rows_step, 0)
+        lax.fori_loop(0, 2, rows_step, 0)
 
 
 def unpack_weights(gathered, head_kind, head_k):
     def spec(i):
-        def index(rh, t, g, kind_ref, k_ref):
+        def index(fx, t, g, kind_ref, k_ref):
             k = k_ref[g * 8 + i]
-            fx = lax.div(rh, 2)
             other = lax.rem(k + fx, 2)
-            return lax.div(k, 2) * 2 + fx, lax.rem(rh, 2), other * 3 + t, 0, 0
-
-        return pl.BlockSpec((None, None, None, ROWS, TILE), index)
+            return lax.div(k, 2) * 2 + fx, 0, other * 3 + t, 0, 0
+
+        return pl.BlockSpec((None, 2, None, ROWS, TILE), index)
 
     return pl.pallas_call(
         unpack_weights_kernel,
-        out_shape=jax.ShapeDtypeStruct((WIDTH, 3 * WIDTH), F32),
+        out_shape=jax.ShapeDtypeStruct((4, ROWS, 3 * WIDTH), F32),
         grid_spec=pltpu.PrefetchScalarGridSpec(
             num_scalar_prefetch=2,
-            grid=(4, 3, 4),
+            grid=(2, 3, 4),
             in_specs=[spec(i) for i in range(8)],
-            out_specs=pl.BlockSpec((ROWS, ROWS), lambda rh, t, g, *_: (rh, t * 4 + g)),
+            out_specs=pl.BlockSpec((2, ROWS, ROWS), lambda fx, t, g, *_: (fx, 0, t * 4 + g)),
         ),
         compiler_params=params(),
         cost_estimate=pl.CostEstimate(flops=20 * 10**9, bytes_accessed=100 * 2**20, transcendentals=0),
         name="unpack_weights",
-    )(head_kind, head_k, *([gathered] * 8))
+    )(head_kind, head_k, *([gathered] * 8)).reshape(WIDTH, 3 * WIDTH)
 
 
 def unpack_out(gathered):
-    def index(rh, c):
-        k = lax.rem(c, 2) * 8 + lax.rem(lax.div(c, 2), 2) * 4 + lax.rem(lax.div(c, 4), 2) * 2 + lax.div(c, 8)
-        return k, rh, 3, 0, 0
+    def index(c):
+        k = lax.rem(c, 2) * 8 + lax.rem(lax.div(c, 2), 2) * 4 + lax.div(c, 8) * 2 + lax.rem(lax.div(c, 4), 2)
+        return k, 0, 0, 0
 
     def body(in_ref, out_ref):
-        out_ref[...] = in_ref[...].reshape(BAND, TILE).astype(F32)
+        out_ref[...] = in_ref[...].astype(F32)
 
     return pl.pallas_call(
         body,
-        out_shape=jax.ShapeDtypeStruct((WIDTH, WIDTH), F32),
-        grid=(2, 16),
-        in_specs=[pl.BlockSpec((None, None, 2, ROWS, TILE), index)],
-        out_specs=pl.BlockSpec((BAND, TILE), lambda rh, c: (rh, c)),
+        out_shape=jax.ShapeDtypeStruct((2, BAND, WIDTH), F32),
+        grid=(16,),
+        in_specs=[pl.BlockSpec((None, 2, BAND, TILE), index)],
+        out_specs=pl.BlockSpec((2, BAND, TILE), lambda c: (0, 0, c)),
         compiler_params=params(),
         cost_estimate=pl.CostEstimate(flops=5 * 10**9, bytes_accessed=24 * 2**20, transcendentals=0),
         name="unpack_out",
-    )(gathered)
+    )(gathered).reshape(WIDTH, WIDTH)
 
 
 def regroup_kernel(f_ref, b_ref, out_ref):
@@ -447,7 +445,6 @@
 
         h_part = trade(h_norm, half, 2, 0, pair_swap)
         h_part = trade(h_part, x_bit, BAND, 3, x_swap)
-        h_all = lax.all_gather(h_part, "sp", axis_index_groups=same_xc).reshape(2 * SEQ, BAND)
         qkv_slots = project(h_norm.reshape(ROWS, WIDTH), w_qkv, b_qkv.astype(F32).reshape(1, 3 * WIDTH), head_kind, head_k, False)
         d_attn_slots = project(d_y_rows, w_out, jnp.zeros((1, WIDTH), F32), head_kind, head_k, True)
         qkv_full = exchange(qkv_slots[0])
@@ -456,7 +453,8 @@
         d_attn = lax.all_to_all(d_attn_slots.reshape(2, DEVS, TILE, TILE), "sp", 1, 1, tiled=True)
         attn_full, lse_full = attend_forward(qkv_full, False)
         o_full = exchange(attn_full)
-        qkv_band, attn_full = lax.optimization_barrier((qkv_band, attn_full))
+        qkv_band, attn_full, h_part = lax.optimization_barrier((qkv_band, attn_full, h_part))
+        h_all = lax.all_gather(h_part, "sp", axis_index_groups=same_xc).reshape(2 * SEQ, BAND)
         attn_band, lse_band = attend_forward(qkv_band, True)
         o_band = exchange(attn_band)
         attn_slots = jnp.stack([o_full, o_band])[:, :, None]
@@ -474,15 +472,15 @@
             take = lax.ppermute(give, "sp", [(i, i ^ 2**step) for i in range(DEVS)])
             return keep + take.astype(F32)
 
-        for step in range(5):
+        for step in (0, 2, 1, 3, 4):
             d_wout = halve(d_wout, step)
+        d_qkv_band = attend_backward(qkv_band, d_attn, attn_band, lse_band, True)
+        p_band = lax.ppermute(d_qkv_band, "sp", x_swap)
+        g_band = exchange(d_qkv_band)
+        lse_full, d_qkv_band = lax.optimization_barrier((lse_full, d_qkv_band))
         d_qkv_full = attend_backward(qkv_full, d_attn, attn_full, lse_full, False)
         p_full = lax.ppermute(d_qkv_full, "sp", x_swap)
         g_full = exchange(d_qkv_full)
-        lse_band, d_qkv_full = lax.optimization_barrier((lse_band, d_qkv_full))
-        d_qkv_band = attend_backward(qkv_band, d_attn, attn_band, lse_band, True)
-        p_band = lax.ppermute(d_qkv_band, "sp", x_swap)
-        g_band = exchange(d_qkv_band)
         d_qkv_slots = jnp.stack([g_full, g_band])
 
         d_own = regroup(d_qkv_full, d_qkv_band)
@@ -494,9 +492,9 @@
         dw_other = lax.dynamic_slice_in_dim(dw_all, ROWS - half * ROWS, ROWS, 2)
         dw_other = lax.ppermute(dw_other, "sp", pair_swap)
         dw_sum = (dw_mine + dw_other).astype(BF16).reshape(6, TILE, ROWS).transpose(0, 2, 1)
-        shares = jnp.concatenate([dw_sum, d_wout.astype(BF16).reshape(2, ROWS, TILE)])
-        shares = lax.all_gather(shares, "sp").reshape(16, 2, 8, ROWS, TILE)
-        d_wout = unpack_out(shares)
+        d_wout = lax.all_gather(d_wout.astype(BF16), "sp").reshape(16, 2, BAND, TILE)
+        d_wout = unpack_out(d_wout)
+        shares = lax.all_gather(dw_sum, "sp").reshape(16, 2, 6, ROWS, TILE)
         d_wqkv = unpack_weights(shares, head_kind, head_k)
 
         d_qkv_tok = unpack(d_qkv_slots, head_kind, head_k)

time: 1340 us -> 1320 us (0.985)
  Pallas kernels: 403 us -> 355 us
  waiting for transfers between devices: 497 us -> 539 us
  blocking collectives: 240 us -> 225 us
    ppermute x5, waiting for transfers between devices: 60.3 us -> 126 us  [halve(): take = lax.ppermute(give, 'sp', [(i, i ^ 2 ** step) for i in range(DEVS)])]
    ppermute x1, waiting for transfers between devices: 0.01 us -> 59.9 us  [layer(): p_full = lax.ppermute(d_qkv_full, 'sp', x_swap)]
    all_to_all x1, waiting for transfers between devices: 56.1 us -> 0.01 us  [layer(): lax.all_to_all(d_attn_slots.reshape(2, DEVS, TILE, TILE), 'sp', 1, 1, til...]
    pallas_call x2, Pallas kernels: 107 us -> 59.4 us  [the longest x1 45.9 us: unpack_weights(): pl.pallas_call(unpack_weights_kernel, out_shape=jax.ShapeDtypeStruct((4,...]
    all_to_all x4, waiting for transfers between devices: 263 us -> 246 us  [exchange(): return lax.all_to_all(slots, 'sp', 0, 0, tiled=True)]
    ppermute x2, waiting for transfers between devices: 52.3 us -> 38.2 us  [trade(): lax.ppermute(lax.dynamic_slice_in_dim(array, width - bit * width, width,...]
  transfers between devices with their start and end apart: 17 -> 18, of which waited for: 9 -> 12; matrix products, arithmetic and copies ran while one was open for 8% -> 8% of each run, Pallas kernels for 20% -> 21%
where the time goes in v2:
time: 1320 us; the launch traced here: 1310 us
  waiting for transfers between devices  539 us (41%)
  Pallas kernels  355 us (27%)
  blocking collectives  225 us (17%)
  matrix products  57.1 us (4%)
  other arithmetic  46.3 us (4%)
  local copies, waits for them, and re-layouts  36.4 us (3%)
  starting transfers between devices  32.5 us (2%)
  between operations  14.5 us (1%)
    all_to_all x4, waiting for transfers between devices, exchange(): return lax.all_to_all(slots, 'sp', 0, 0, tiled=True)  246 us
    all_to_all x2, blocking collectives, exchange(): return lax.all_to_all(slots, 'sp', 0, 0, tiled=True)  186 us
    ppermute x5, waiting for transfers between devices, halve(): take = lax.ppermute(give, 'sp', [(i, i ^ 2 ** step) for i in range(DEVS)])  126 us
    pallas_call x2, Pallas kernels, attend_backward(): pl.pallas_call(lambda *refs: backward_kernel(*refs, banded=banded, scale=...  120 us
    pallas_call x2, Pallas kernels, attend_forward(): pl.pallas_call(lambda *refs: forward_kernel(*refs, banded=banded, scale2=...  94.6 us
    ppermute x1, waiting for transfers between devices, layer(): p_band = lax.ppermute(d_qkv_band, 'sp', x_swap)  65.4 us
    ppermute x1, waiting for transfers between devices, layer(): p_full = lax.ppermute(d_qkv_full, 'sp', x_swap)  59.9 us
    dot_general x5, matrix products, dot(): return lax.dot_general(a, b, dims, preferred_element_type=F32)  57.1 us
  transfers between devices with their start and end apart: 18, of which 12 were waited for; matrix products, arithmetic and copies ran while one was open for 8% of the time, Pallas kernels for 21%

profile of v2, /device:TPU:0, one launch (start us, length us, event | category | flops | bytes accessed | tf_op | source)
XLA Modules:
  0.0 1305.2 jit_solution(17886390935519890945)
XLA Ops:
  15.1 33.1 %project.2 = bf16[2,32,3,128,128]{4,3,2,1,0:T(8,128)(2,1)} custom-call(s32[32]{0:T(128)} %kind_ref.5, s32[32]{0:T(128)} %compare_select_fusion.refs_1_.k_ref, bf16[512,2048]{1,0:T(8,128)(2,1)} %bitcast.60, bf16[2048,6144]{1,0:T(8,128)(2,1)} %refs_3_.2, f32[1,6144]{1,0:T(1,128)} %bitcast.70), custom_call_target="tpu_custom_call" | custom-call | flops 12884901888 | bytes 25165824 | tf_op jit(solution)/shard_map/project/pallas_call | solution.py:95
  65.3 69.9 %all-to-all-done.refs_0_.refs_1_.refs_2_ = bf16[32,3,128,128]{3,2,1,0:T(8,128)(2,1)} async-done(((bf16[32,3,128,128]{3,2,1,0:T(8,128)(2,1)}), bf16[32,3,128,128]{3,2,1,0:T(8,128)(2,1)}, u32[]{:S(2)}, u32[]{:S(2)}) %all-to-all-start) | async-done | bytes 3145760 | tf_op jit(solution)/shard_map/all_to_all | solution.py:420
  142.5 13.5 %project.3 = bf16[2,32,1,128,128]{4,3,2,1,0:T(8,128)(2,1)} custom-call(s32[32]{0:T(128)} %kind_ref.5, s32[32]{0:T(128)} %compare_select_fusion.refs_1_.k_ref, bf16[512,2048]{1,0:T(8,128)(2,1)} %bitcast.66, bf16[2048,2048]{1,0:T(8,128)(2,1)} %refs_3_.3, f32[1,2048]{1,0:T(1,128)} %broadcast_in_dim.31.refs_4_), custom_call_target="tpu_custom_call" | custom-call | flops 4294967296 | bytes 8388608 | tf_op jit(solution)/shard_map/project/pallas_call | solution.py:95
  155.9 38.2 %collective-permute-done.1 = bf16[2,2,128,1024]{3,2,1,0:T(8,128)(2,1)S(1)} collective-permute-done((bf16[2,2,128,1024]{3,2,1,0:T(8,128)(2,1)S(1)}, bf16[2,2,128,1024]{3,2,1,0:T(8,128)(2,1)S(1)}, u32[]{:S(2)}, u32[]{:S(2)}) %collective-permute-start.1) | collective-permute-done | bytes 1048608 | tf_op jit(solution)/shard_map/ppermute | solution.py:443
  195.7 56.6 %forward_full.1 = (bf16[32,128,128]{2,1,0:T(8,128)(2,1)}, f32[16,512]{1,0:T(8,128)}) custom-call(bf16[32,3,128,128]{3,2,1,0:T(8,128)(2,1)} %all-to-all-done.refs_0_.refs_1_.refs_2_, bf16[32,3,128,128]{3,2,1,0:T(8,128)(2,1)} %all-to-all-done.refs_0_.refs_1_.refs_2_, bf16[32,3,128,128]{3,2,1,0:T(8,128)(2,1)} %all-to-all-done.refs_0_.refs_1_.refs_2_), custom_call_target="tpu_custom_call" | custom-call | flops 35999997952 | bytes 4194304 | tf_op jit(solution)/shard_map/forward_full/pallas_call | solution.py:323
  252.4 38.0 %forward_band.1 = (bf16[32,128,128]{2,1,0:T(8,128)(2,1)}, f32[16,512]{1,0:T(8,128)}) custom-call(bf16[32,3,128,128]{3,2,1,0:T(8,128)(2,1)} %all-to-all-done.2.refs_0_.refs_1_.refs_2_, bf16[32,3,128,128]{3,2,1,0:T(8,128)(2,1)} %all-to-all-done.2.refs_0_.refs_1_.refs_2_, bf16[32,3,128,128]{3,2,1,0:T(8,128)(2,1)} %all-to-all-done.2.refs_0_.refs_1_.refs_2_), custom_call_target="tpu_custom_call" | custom-call | flops 20999999488 | bytes 4194304 | tf_op jit(solution)/shard_map/forward_band/pallas_call | solution.py:323
  290.4 60.5 %all_to_all.35 = bf16[32,128,128]{2,1,0:T(8,128)(2,1)S(1)} all-to-all(bf16[32,128,128]{2,1,0:T(8,128)(2,1)} %get-tuple-element.22.refs_4_), channel_id=1, replica_groups=mesh['sp'=32] {'sp'}, dimensions={0} | all-to-all | bytes 2097152 | tf_op jit(solution)/shard_map/all_to_all | solution.py:420
  354.6 51.8 %all-to-all-done.1 = bf16[32,128,128]{2,1,0:T(8,128)(2,1)S(1)} async-done(((bf16[32,128,128]{2,1,0:T(8,128)(2,1)}), bf16[32,128,128]{2,1,0:T(8,128)(2,1)S(1)}, u32[]{:S(2)}, u32[]{:S(2)}) %all-to-all-start.1) | async-done | bytes 1048608 | tf_op jit(solution)/shard_map/all_to_all | solution.py:420
  453.1 70.5 %collective-permute-done.6 = bf16[1024,1024]{1,0:T(8,128)(2,1)} collective-permute-done((bf16[1024,1024]{1,0:T(8,128)(2,1)}, bf16[1024,1024]{1,0:T(8,128)(2,1)}, u32[]{:S(2)}, u32[]{:S(2)}) %collective-permute-start.6) | collective-permute-done | bytes 2097184 | tf_op jit(solution)/shard_map/ppermute | solution.py:472
  530.5 25.8 %collective-permute-done.7 = bf16[1024,512]{1,0:T(8,128)(2,1)} collective-permute-done((bf16[1024,512]{1,0:T(8,128)(2,1)S(1)}, bf16[1024,512]{1,0:T(8,128)(2,1)}, u32[]{:S(2)}, u32[]{:S(2)}) %collective-permute-start.7) | collective-permute-done | bytes 1048608 | tf_op jit(solution)/shard_map/ppermute | solution.py:472
  561.6 11.4 collective-permute-done.8
  576.9 10.7 collective-permute-done.9
  589.6 49.7 %backward_band.1.b_ref = bf16[32,3,128,128]{3,2,1,0:T(8,128)(2,1)} custom-call(bf16[32,3,128,128]{3,2,1,0:T(8,128)(2,1)} %all-to-all-done.2.refs_0_.refs_1_.refs_2_, bf16[32,3,128,128]{3,2,1,0:T(8,128)(2,1)} %all-to-all-done.2.refs_0_.refs_1_.refs_2_, bf16[32,3,128,128]{3,2,1,0:T(8,128)(2,1)} %all-to-all-done.2.refs_0_.refs_1_.refs_2_, ...), custom_call_target="tpu_custom_call" | custom-call | flops 41999998976 | bytes 8388608 | tf_op jit(solution)/shard_map/backward_band/pallas_call | solution.py:400
  639.3 70.1 %backward_full.1.f_ref = bf16[32,3,128,128]{3,2,1,0:T(8,128)(2,1)} custom-call(bf16[32,3,128,128]{3,2,1,0:T(8,128)(2,1)} %all-to-all-done.refs_0_.refs_1_.refs_2_, bf16[32,3,128,128]{3,2,1,0:T(8,128)(2,1)} %all-to-all-done.refs_0_.refs_1_.refs_2_, bf16[32,3,128,128]{3,2,1,0:T(8,128)(2,1)} %all-to-all-done.refs_0_.refs_1_.refs_2_, ...), custom_call_target="tpu_custom_call" | custom-call | flops 71999995904 | bytes 8388608 | tf_op jit(solution)/shard_map/backward_full/pallas_call | solution.py:400
  720.8 59.9 %collective-permute-done.2.f_ref = bf16[32,3,128,128]{3,2,1,0:T(8,128)(2,1)} collective-permute-done((bf16[32,3,128,128]{3,2,1,0:T(8,128)(2,1)}, bf16[32,3,128,128]{3,2,1,0:T(8,128)(2,1)}, u32[]{:S(2)}, u32[]{:S(2)}) %collective-permute-start.2) | collective-permute-done | bytes 3145760 | tf_op jit(solution)/shard_map/ppermute | solution.py:482
  780.7 65.4 %collective-permute-done.3.b_ref = bf16[32,3,128,128]{3,2,1,0:T(8,128)(2,1)} collective-permute-done((bf16[32,3,128,128]{3,2,1,0:T(8,128)(2,1)S(1)}, bf16[32,3,128,128]{3,2,1,0:T(8,128)(2,1)}, u32[]{:S(2)}, u32[]{:S(2)}) %collective-permute-start.3) | collective-permute-done | bytes 3145760 | tf_op jit(solution)/shard_map/ppermute | solution.py:478
  855.5 12.2 convolution_bitcast_fusion.1
  886.3 125.4 %all_to_all.36 = bf16[32,3,128,128]{3,2,1,0:T(8,128)(2,1)S(1)} all-to-all(bf16[32,3,128,128]{3,2,1,0:T(8,128)(2,1)} %backward_band.1.b_ref), channel_id=1, replica_groups=mesh['sp'=32] {'sp'}, dimensions={0} | all-to-all | bytes 6291456 | tf_op jit(solution)/shard_map/all_to_all | solution.py:420
  1026.5 123.8 %all-to-all-done.5 = bf16[32,3,128,128]{3,2,1,0:T(8,128)(2,1)} async-done(((bf16[32,3,128,128]{3,2,1,0:T(8,128)(2,1)}), bf16[32,3,128,128]{3,2,1,0:T(8,128)(2,1)}, u32[]{:S(2)}, u32[]{:S(2)}) %all-to-all-start.5) | async-done | bytes 3145760 | tf_op jit(solution)/shard_map/all_to_all | solution.py:420
  1155.6 10.8 unpack.3
  1166.3 21.2 %fusion.21 = (f32[2048]{0:T(1024)S(1)}, f32[512,2048]{1,0:T(8,128)}) fusion(bf16[512,6144]{1,0:T(8,128)(2,1)} %unpack.3, bf16[2048,6144]{1,0:T(8,128)(2,1)} %refs_3_.2), kind=kOutput, calls=%fused_computation.62 | convolution fusion | flops 12888045568 | bytes 35659776 | tf_op jit(solution)/shard_map/dot_general | solution.py:28
  1200.2 38.9 %all-reduce = (f32[2048]{0:T(1024)}, f32[2048]{0:T(1024)}, f32[6144]{0:T(1024)}, f32[2048]{0:T(1024)}) all-reduce(f32[2048]{0:T(1024)S(1)} %get-tuple-element.30, f32[2048]{0:T(1024)S(1)} %get-tuple-element.45, f32[6144]{0:T(1024)S(1)} %convert_reduce_fusion, f32[2048]{0:T(1024)S(1)} %get-tuple-element.38), channel_id=1, replica_groups=mesh['sp'=32] {'sp'}, use_global_device_ids=true, to_apply=%region_6.7 | all-reduce | flops 12288 | bytes 98304 | tf_op jit(solution)/shard_map/psum | solution.py:506
  1239.1 13.5 %unpack_out.1 = f32[2,1024,2048]{2,1,0:T(8,128)} custom-call(bf16[16,2,1024,128]{3,2,1,0:T(8,128)(2,1)} %bitcast.59), custom_call_target="tpu_custom_call" | custom-call | flops 5000000000 | bytes 25165824 | tf_op jit(solution)/shard_map/unpack_out/pallas_call | solution.py:204
  1252.6 45.9 %unpack_weights.1 = f32[4,512,6144]{2,1,0:T(8,128)} custom-call(s32[32]{0:T(128)} %kind_ref.5, s32[32]{0:T(128)} %compare_select_fusion.refs_1_.k_ref, bf16[16,2,6,512,128]{4,3,2,1,0:T(8,128)(2,1)} %bitcast.44, bf16[16,2,6,512,128]{4,3,2,1,0:T(8,128)(2,1)} %bitcast.45, bf16[16,2,6,512,128]{4,3,2,1,0:T(8,128)(2,1)} %bitcast.46, ...), custom_call_target="tpu_custom_call" | custom-call | flops 20000000000 | bytes 104857600 | tf_op jit(solution)/shard_map/unpack_weights/pallas_call | solution.py:181
  (136 shorter events, 174.0 us)
Async XLA Ops:
  56.5 78.8 %all-to-all-start = ((bf16[32,3,128,128]{3,2,1,0:T(8,128)(2,1)}), bf16[32,3,128,128]{3,2,1,0:T(8,128)(2,1)}, u32[]{:S(2)}, u32[]{:S(2)}) async-start(bf16[32,3,128,128]{3,2,1,0:T(8,128)(2,1)} %get-tuple-element.36), calls=%async_computation | async-start | bytes 6291456 | tf_op jit(solution)/shard_map/all_to_all | solution.py:420
  65.1 74.4 %collective-permute-start = (bf16[2,128,2048]{2,1,0:T(8,128)(2,1)}, bf16[2,128,2048]{2,1,0:T(8,128)(2,1)S(1)}, u32[]{:S(2)}, u32[]{:S(2)}) collective-permute-start(bf16[2,128,2048]{2,1,0:T(8,128)(2,1)} %get-tuple-element.44), channel_id=1, source_target_pairs={{0,1},{1,0},{2,3},{3,2},{4,5},{5,4},{6,7},{7,6},{8,9},{9,8},{10,11... | collective-permute-start | bytes 3145736 | tf_op jit(solution)/shard_map/ppermute | solution.py:443
  135.3 117.1 %all-to-all-start.2 = ((bf16[32,3,128,128]{3,2,1,0:T(8,128)(2,1)}), bf16[32,3,128,128]{3,2,1,0:T(8,128)(2,1)}, u32[]{:S(2)}, u32[]{:S(2)}) async-start(bf16[32,3,128,128]{3,2,1,0:T(8,128)(2,1)} %get-tuple-element.37), calls=%async_computation.2 | async-start | bytes 6291456 | tf_op jit(solution)/shard_map/all_to_all | solution.py:420
  139.4 716.1 %all-gather.7.cloned.1.call-start = ((), (), s32[]{:S(2)}) async-start(), calls=%async_computation.7 | async-start | bytes 18874368 | tf_op jit(solution)/shard_map/all_gather | solution.py:457
  140.1 54.0 %collective-permute-start.1 = (bf16[2,2,128,1024]{3,2,1,0:T(8,128)(2,1)S(1)}, bf16[2,2,128,1024]{3,2,1,0:T(8,128)(2,1)S(1)}, u32[]{:S(2)}, u32[]{:S(2)}) collective-permute-start(bf16[2,2,128,1024]{3,2,1,0:T(8,128)(2,1)S(1)} %get-tuple-element.42), channel_id=1, source_target_pairs={{0,2},{1,3},{2,0},{3,1},{4,6},{5,7},{6,4},{7,5},{8,10},{9,11},{10,... | collective-permute-start | bytes 3145736 | tf_op jit(solution)/shard_map/ppermute | solution.py:443
  350.8 55.5 %all-to-all-start.1 = ((bf16[32,128,128]{2,1,0:T(8,128)(2,1)}), bf16[32,128,128]{2,1,0:T(8,128)(2,1)S(1)}, u32[]{:S(2)}, u32[]{:S(2)}) async-start(bf16[32,128,128]{2,1,0:T(8,128)(2,1)} %get-tuple-element.24.refs_4_), calls=%async_computation.1 | async-start | bytes 2097152 | tf_op jit(solution)/shard_map/all_to_all | solution.py:420
  428.1 7.5 collective-permute-start.5
  446.6 77.0 %collective-permute-start.6 = (bf16[1024,1024]{1,0:T(8,128)(2,1)}, bf16[1024,1024]{1,0:T(8,128)(2,1)}, u32[]{:S(2)}, u32[]{:S(2)}) collective-permute-start(bf16[1024,1024]{1,0:T(8,128)(2,1)} %dynamic-slice_convert_fusion.1), channel_id=1, source_target_pairs={{0,4},{1,5},{2,6},{3,7},{4,0},{5,1},{6,2},{7,3},{8,12},{9,13},{10,... | collective-permute-start | bytes 6291464 | tf_op jit(solution)/shard_map/ppermute | solution.py:472
  449.8 125.7 %all-to-all-start.4 = ((bf16[2,32,128,128]{3,2,0,1:T(8,128)(2,1)}), bf16[2,32,128,128]{3,2,0,1:T(8,128)(2,1)S(1)}, u32[]{:S(2)}, u32[]{:S(2)}) async-start(bf16[2,32,128,128]{3,2,0,1:T(8,128)(2,1)} %copy.22), calls=%async_computation.4 | async-start | bytes 4194304 | tf_op jit(solution)/shard_map/all_to_all | solution.py:453
  453.0 786.1 %all-gather.11.cloned.1.call-start = ((), (), s32[]{:S(2)}) async-start(), calls=%async_computation.9 | async-start | bytes 8650752 | tf_op jit(solution)/shard_map/all_gather | solution.py:495
  529.3 27.0 %collective-permute-start.7 = (bf16[1024,512]{1,0:T(8,128)(2,1)S(1)}, bf16[1024,512]{1,0:T(8,128)(2,1)}, u32[]{:S(2)}, u32[]{:S(2)}) collective-permute-start(bf16[1024,512]{1,0:T(8,128)(2,1)S(1)} %dynamic-slice_convert_fusion.2), channel_id=1, source_target_pairs={{0,2},{1,3},{2,0},{3,1},{4,6},{5,7},{6,4},{7,5},{8,10},{9,11},{10,... | collective-permute-start | bytes 3145736 | tf_op jit(solution)/shard_map/ppermute | solution.py:472
  559.9 13.0 collective-permute-start.8
  574.5 13.1 %collective-permute-start.9 = (bf16[1024,128]{1,0:T(8,128)(2,1)S(1)}, bf16[1024,128]{1,0:T(8,128)(2,1)}, u32[]{:S(2)}, u32[]{:S(2)}) collective-permute-start(bf16[1024,128]{1,0:T(8,128)(2,1)S(1)} %dynamic-slice_convert_fusion.4), channel_id=1, source_target_pairs={{0,16},{1,17},{2,18},{3,19},{4,20},{5,21},{6,22},{7,23},{8,24},{9,... | collective-permute-start | bytes 786440 | tf_op jit(solution)/shard_map/ppermute | solution.py:472
  589.4 663.2 %all-gather.9.cloned.1.call-start = ((), (), s32[]{:S(2)}) async-start(), calls=%async_computation.8 | async-start | bytes 25952256 | tf_op jit(solution)/shard_map/all_gather | solution.py:497
  639.3 71.1 %copy-start.9 = (bf16[32,3,128,128]{3,2,1,0:T(8,128)(2,1)S(1)}, bf16[32,3,128,128]{3,2,1,0:T(8,128)(2,1)}, u32[]{:S(2)}) copy-start(bf16[32,3,128,128]{3,2,1,0:T(8,128)(2,1)} %backward_band.1.b_ref) | copy-start | bytes 9437188
  709.4 71.3 %collective-permute-start.2 = (bf16[32,3,128,128]{3,2,1,0:T(8,128)(2,1)}, bf16[32,3,128,128]{3,2,1,0:T(8,128)(2,1)}, u32[]{:S(2)}, u32[]{:S(2)}) collective-permute-start(bf16[32,3,128,128]{3,2,1,0:T(8,128)(2,1)} %backward_full.1.f_ref), channel_id=1, source_target_pairs={{0,2},{1,3},{2,0},{3,1},{4,6},{5,7},{6,4},{7,5},{8,10},{9,11},{10,... | collective-permute-start | bytes 9437192 | tf_op jit(solution)/shard_map/ppermute | solution.py:482
  710.4 135.7 %collective-permute-start.3 = (bf16[32,3,128,128]{3,2,1,0:T(8,128)(2,1)S(1)}, bf16[32,3,128,128]{3,2,1,0:T(8,128)(2,1)}, u32[]{:S(2)}, u32[]{:S(2)}) collective-permute-start(bf16[32,3,128,128]{3,2,1,0:T(8,128)(2,1)S(1)} %copy-done.9), channel_id=1, source_target_pairs={{0,2},{1,3},{2,0},{3,1},{4,6},{5,7},{6,4},{7,5},{8,10},{9,11},{10,... | collective-permute-start | bytes 9437192 | tf_op jit(solution)/shard_map/ppermute | solution.py:478
  855.5 12.3 copy-start.26
  855.5 14.1 %copy-start.27 = (bf16[384,8192]{1,0:T(8,128)(2,1)S(1)}, bf16[384,8192]{1,0:T(8,128)(2,1)}, u32[]{:S(2)}) copy-start(bf16[384,8192]{1,0:T(8,128)(2,1)} %regroup.3) | copy-start | bytes 18874372
  877.7 3.8 collective-permute-start.4
  1011.8 138.6 %all-to-all-start.5 = ((bf16[32,3,128,128]{3,2,1,0:T(8,128)(2,1)}), bf16[32,3,128,128]{3,2,1,0:T(8,128)(2,1)}, u32[]{:S(2)}, u32[]{:S(2)}) async-start(bf16[32,3,128,128]{3,2,1,0:T(8,128)(2,1)} %backward_full.1.f_ref), calls=%async_computation.5 | async-start | bytes 6291456 | tf_op jit(solution)/shard_map/all_to_all | solution.py:420
  1166.3 21.3 %copy-start.1 = (bf16[4,128,2048]{2,1,0:T(8,128)(2,1)S(1)}, bf16[4,128,2048]{2,1,0:T(8,128)(2,1)}, u32[]{:S(2)}) copy-start(bf16[4,128,2048]{2,1,0:T(8,128)(2,1)} %param.9) | copy-start | bytes 6291460
  1166.3 21.3 %copy-start.14 = (f32[2048]{0:T(1024)S(1)}, f32[2048]{0:T(1024)}, u32[]{:S(2)}) copy-start(f32[2048]{0:T(1024)} %copy-done.13) | copy-start | bytes 24580
  1166.3 21.3 %copy-start.16 = (f32[4,128]{1,0:T(4,128)S(1)}, f32[4,128]{1,0:T(4,128)}, u32[]{:S(2)}) copy-start(f32[4,128]{1,0:T(4,128)} %copy-done.15) | copy-start | bytes 6148
  (24 other events, 94.2 us)
Sparse Core Ops, SparseCore 0:
  252.5 308.6 all-gather.6
  589.5 75.3 all-gather.10
  886.4 265.7 all-gather.8
